TPU v7x, 256 devices: a 2x2x32 block of a 4x8x32 slice. The times are simulated.
256 devices in a mesh: tm: 4 (over y, x), slab: 64 (over z, core).
Axes of the slice: x: 2, y: 2, z: 32, core: 2. Of those that a mesh axis runs over, the one named last changes fastest.
The devices are a block of a 4x8x32 slice.
Arguments:
- volumes: bfloat16 [32, 4096, 64, 128], P('tm', 'slab'), parts along dimension 0, may hold values from -6 to 6
- pair_fields: int32 [8, 1024], P(None, ('tm', 'slab')), parts along dimension 1, may hold values from -16 to 64, as said below
- pair_counts: int32 [256], P(('tm', 'slab')), parts along dimension 0, may hold values from 1 to 4, as said below
Outputs:
- correlation: float32 [1024, 512], P(('tm', 'slab')), parts along dimension 0
- shifts: float32 [3, 1024], P(None, ('tm', 'slab')), parts along dimension 1
- normal_sums: float32 [32, 4, 4], P('tm'), parts along dimension 0
- rhs_sums: float32 [32, 4, 3], P('tm'), parts along dimension 0
There are 4 independent parts, one for each index of `tm`. A program takes and returns all parts, laid end to end along the dimension named above; each array names one. Nothing has to cross between parts.
Inputs may be any that keep to these rules, and one draw needn't show every extreme that they name: `pair_fields`: column p belongs to slab p // 4. Rows: first view; x anchor of its block (0 to 64); second view, the first plus or minus one modulo 8; slab offset of the second block (-1, 0 or 1, never leading outside the volume; 0 in dead columns); x anchor of the second block (0 to 64); window offsets along z, y, x (-16 to 8). Among one slab's live pairs at most 2 have slab offset 1 and at most 2 have -1; in every draw some slab has exactly 2 of each. The first pair of the first slab has slab offset 1 and the first pair of the last slab has -1. `pair_counts`: the live pairs of a slab fill its first slots; in every draw some slab has 4.
All inputs are finite; a program needn't handle non-finite values.
Results may differ from a plain program's by a relative error of at most 0.0003.
Values may be sent and summed in bfloat16 or wider, within the bound.
No kernel may reach another device: no remote copies, remote signals or barrier semaphores. Data moves between devices by JAX's collectives and lax.ppermute only.
A program may use at most 128 MiB of HBM per device.

v0:
```python
import math

import jax
import jax.numpy as jnp
from jax import lax
from jax.sharding import PartitionSpec as P

WIN = 8
NBR = 2


TWO_PI = 2.0 * math.pi
EPSILON = 1e-06
PRECISE = lax.Precision.HIGHEST


def passed_along(value, axis, steps):
    count = lax.axis_size(axis)
    leading, last = (max(0, -steps), min(count, count - steps))
    return lax.ppermute(value, axis, [(source, source + steps) for source in range(leading, last)])


def sent_to_all(shard, axis):
    devices = lax.axis_size(axis)
    return lax.all_to_all(
        jnp.broadcast_to(shard[None], (devices, *shard.shape)), axis, 0, 0, tiled=True
    )


def taken_together(shard, axis):
    everything = sent_to_all(shard, axis)
    return jnp.sum(everything, axis=0)


def packed_total(arrays, axis):
    ends = [0]
    for a in arrays:
        ends.append(ends[-1] + a.size)
    so_far = taken_together(jnp.concatenate([a.ravel() for a in arrays]), axis)
    return tuple((so_far[b:e].reshape(a.shape) for a, b, e in zip(arrays, ends, ends[1:])))


def angle_pair(first_ids, second_ids, block_edge):
    product = jnp.mod(first_ids[:, None] * second_ids[None, :], block_edge).astype(jnp.float32)
    angles = TWO_PI * product / block_edge
    return (jnp.cos(angles), jnp.sin(angles))


def swap_parts(values, block_edge, sign):
    return jnp.concatenate(
        [-sign * values[..., block_edge:], sign * values[..., :block_edge]], axis=-1
    )


def spectrum(slab_rows, anchor, block_edge):
    window_rows = lax.dynamic_slice_in_dim(slab_rows, anchor, block_edge, 2)
    cell_ids = jnp.arange(block_edge, dtype=jnp.int32)
    lane_ids = jnp.arange(2 * block_edge, dtype=jnp.int32)
    product = jnp.mod(cell_ids[:, None] * (lane_ids[None, :] % block_edge), block_edge).astype(
        jnp.float32
    )
    angles = TWO_PI * product / block_edge
    dft_table = jnp.where(lane_ids[None, :] < block_edge, jnp.cos(angles), -jnp.sin(angles))
    flat_rows = window_rows.reshape(-1, block_edge).astype(jnp.float32)
    spectra = jnp.dot(flat_rows, dft_table, precision=PRECISE, preferred_element_type=jnp.float32)
    spectra = spectra.reshape(block_edge, block_edge, 2 * block_edge)
    cos_part, sin_part = angle_pair(cell_ids, cell_ids, block_edge)
    stacked = jnp.concatenate([cos_part, sin_part], axis=0)
    mixed = jnp.einsum("zyc,ky->zkc", spectra, stacked, precision=PRECISE)
    spectra = mixed[:, :block_edge] + swap_parts(mixed[:, block_edge:], block_edge, -1.0)
    mixed = jnp.einsum("zyc,kz->kyc", spectra, stacked, precision=PRECISE)
    return mixed[:block_edge] + swap_parts(mixed[block_edge:], block_edge, -1.0)


def window_corr(ratio_parts, offsets, block_edge):
    freq_ids = jnp.arange(block_edge, dtype=jnp.int32)
    window_steps = jnp.arange(WIN, dtype=jnp.int32)
    cos_z, sin_z = angle_pair(offsets[0] + window_steps, freq_ids, block_edge)
    mixed = jnp.einsum(
        "zyc,iz->iyc", ratio_parts, jnp.concatenate([cos_z, sin_z], axis=0), precision=PRECISE
    )
    partial_z = mixed[:WIN] + swap_parts(mixed[WIN:], block_edge, 1.0)
    cos_y, sin_y = angle_pair(offsets[1] + window_steps, freq_ids, block_edge)
    mixed = jnp.einsum(
        "iyc,jy->ijc", partial_z, jnp.concatenate([cos_y, sin_y], axis=0), precision=PRECISE
    )
    partial_y = mixed[:, :WIN] + swap_parts(mixed[:, WIN:], block_edge, 1.0)
    cos_x, sin_x = angle_pair(offsets[2] + window_steps, freq_ids, block_edge)
    real_table = jnp.concatenate([jnp.transpose(cos_x), -jnp.transpose(sin_x)], axis=0)
    values = jnp.einsum("ijc,ck->ijk", partial_y, real_table, precision=PRECISE)
    return values / block_edge**1.5


def pair_term(rows_a, rows_b, column, slab_pos, slab_count, view_count):
    block_edge = rows_a.shape[0]
    spec_a = spectrum(rows_a, column[1], block_edge)
    spec_b = spectrum(rows_b, column[4], block_edge)
    a_real = spec_a[..., :block_edge]
    a_imag = spec_a[..., block_edge:]
    b_real = spec_b[..., :block_edge]
    b_imag = spec_b[..., block_edge:]
    c_real = a_real * b_real + a_imag * b_imag
    c_imag = a_imag * b_real - a_real * b_imag
    magnitude = jnp.sqrt(c_real * c_real + c_imag * c_imag)
    denominator = magnitude + (jnp.mean(magnitude) + EPSILON)
    ratio_parts = jnp.concatenate([c_real / denominator, c_imag / denominator], axis=-1)
    values = window_corr(ratio_parts, (column[5], column[6], column[7]), block_edge)
    weight = values * values
    energy = jnp.mean(weight)
    steps_f = jnp.arange(WIN, dtype=jnp.float32)
    along_z = (column[5].astype(jnp.float32) + steps_f)[:, None, None]
    along_y = (column[6].astype(jnp.float32) + steps_f)[None, :, None]
    along_x = (column[7].astype(jnp.float32) + steps_f)[None, None, :]
    shift_vec = jnp.stack(
        [jnp.mean(weight * along_z), jnp.mean(weight * along_y), jnp.mean(weight * along_x)]
    ) / (energy + EPSILON)
    center = jnp.stack(
        [
            (slab_pos.astype(jnp.float32) * block_edge + 0.5 * block_edge)
            / (block_edge * slab_count),
            jnp.ones((), jnp.float32) * 0.5,
            (column[1].astype(jnp.float32) + 0.5 * block_edge) / (2.0 * block_edge),
            jnp.ones((), jnp.float32),
        ]
    )
    view_ids = jnp.arange(view_count, dtype=jnp.int32)
    hit_a = (view_ids == column[0]).astype(jnp.float32)
    hit_b = (view_ids == column[2]).astype(jnp.float32)
    outer_hh = energy * center[:, None] * center[None, :]
    normal_part = (hit_a + hit_b)[:, None, None] * outer_hh[None]
    rhs_part = (hit_a - hit_b)[:, None, None] * (energy * center[:, None] * shift_vec[None, :])[
        None
    ]
    return (values.reshape(-1), shift_vec, normal_part, rhs_part)


def request_rank(fields, counts, direction):
    slot_ids = jnp.arange(fields.shape[1], dtype=jnp.int32)
    wanted = (fields[3] == direction) & (slot_ids < counts[0])
    return (jnp.cumsum(wanted.astype(jnp.int32)) - 1, wanted)


def requested(volumes, fields, counts, direction, capacity):
    rank_now, wanted = request_rank(fields, counts, direction)
    rank_levels = jnp.arange(capacity, dtype=jnp.int32)
    selector = (wanted[None, :] & (rank_now[None, :] == rank_levels[:, None])).astype(jnp.int32)
    view_pick = jnp.sum(selector * fields[2][None, :], axis=1)
    return volumes[view_pick]


def on_device(volumes, pair_fields, pair_counts):
    view_count = volumes.shape[0]
    slot_cap = pair_fields.shape[1]
    window_cells = WIN**3
    slab_count = lax.axis_size("slab")
    own_index = lax.axis_index("slab")
    live_count = pair_counts[0]
    below_fields, below_count = passed_along((pair_fields, pair_counts), "slab", 1)
    above_fields, above_count = passed_along((pair_fields, pair_counts), "slab", -1)
    from_above = passed_along(requested(volumes, below_fields, below_count, 1, NBR), "slab", -1)
    from_below = passed_along(requested(volumes, above_fields, above_count, -1, NBR), "slab", 1)
    rank_up, wanted_up = request_rank(pair_fields, pair_counts, 1)
    rank_down, wanted_down = request_rank(pair_fields, pair_counts, -1)

    def rows_b_of(column, slot_index):
        local_rows = volumes[column[2]]
        upper_rows = from_above[jnp.clip(rank_up[slot_index], 0, NBR - 1)]
        lower_rows = from_below[jnp.clip(rank_down[slot_index], 0, NBR - 1)]
        return jnp.where(
            column[3] == 1, upper_rows, jnp.where(column[3] == -1, lower_rows, local_rows)
        )

    def own_step(slot_index, running):
        corr_all, shift_all, normal, rhs = running
        column = lax.dynamic_index_in_dim(pair_fields, slot_index, 1, keepdims=False)
        corr_flat, shift_vec, normal_part, rhs_part = pair_term(
            volumes[column[0]],
            rows_b_of(column, slot_index),
            column,
            own_index,
            slab_count,
            view_count,
        )
        corr_all = lax.dynamic_update_index_in_dim(corr_all, corr_flat, slot_index, 0)
        shift_all = lax.dynamic_update_index_in_dim(shift_all, shift_vec, slot_index, 1)
        return (corr_all, shift_all, normal + normal_part, rhs + rhs_part)

    start_state = (
        jnp.zeros((slot_cap, window_cells), jnp.float32),
        jnp.zeros((3, slot_cap), jnp.float32),
        jnp.zeros((view_count, 4, 4), jnp.float32),
        jnp.zeros((view_count, 4, 3), jnp.float32),
    )
    corr_all, shift_all, normal, rhs = lax.fori_loop(
        jnp.int32(0), live_count, own_step, start_state
    )
    normal, rhs = packed_total((normal, rhs), "slab")
    pair_total = float(slot_cap * slab_count)
    return (corr_all, shift_all, normal / pair_total, rhs / pair_total)


def solution(mesh):
    in_specs = (P("tm", "slab", None, None), P(None, ("tm", "slab")), P(("tm", "slab")))
    out_specs = (
        P(("tm", "slab"), None),
        P(None, ("tm", "slab")),
        P("tm", None, None),
        P("tm", None, None),
    )
    return jax.shard_map(
        on_device, mesh=mesh, in_specs=in_specs, out_specs=out_specs, check_vma=False
    )
```

profile of v0, /device:TPU:38, one launch (start us, length us, event | category | flops | bytes accessed | tf_op | source)
XLA Modules:
  0.0 405.5 jit_solution(18079704692456760902)
XLA Ops:
  0.6 1.3 collective-permute-start.3
  1.9 3.1 collective-permute-start
  5.0 1.3 collective-permute-start.4
  6.3 4.9 %collective-permute-start.1 = (s32[1]{0:T(128)}, s32[1]{0:T(128)}, u32[]{:S(2)}, u32[]{:S(2)}) collective-permute-start(s32[1]{0:T(128)} %param.7), channel_id=1, source_target_pairs={{0,1},{1,2},{2,3},{3,4},{4,5},{5,6},{6,7},{7,8},{8,9},{9,10},{10,1... | collective-permute-start | bytes 20 | tf_op jit(solution)/shard_map/ppermute | solution.py:20
  12.5 5.5 %gather_fusion.1 = bf16[2,64,64,128]{3,2,1,0:T(8,128)(2,1)} fusion(bf16[8,64,64,128]{3,2,1,0:T(8,128)(2,1)} %param.5, s32[1024]{0:T(1024)S(1)} %pad_clamp_fusion), kind=kCustom, calls=%fused_computation.1 | custom fusion | bytes 4194312 | tf_op jit(solution)/shard_map/gather | solution.py:148
  18.0 3.2 collective-permute-start.5
  21.2 0.9 convert_reduce_fusion.1
  22.6 5.5 %gather_fusion = bf16[2,64,64,128]{3,2,1,0:T(8,128)(2,1)} fusion(bf16[8,64,64,128]{3,2,1,0:T(8,128)(2,1)} %param.5, s32[1024]{0:T(1024)S(1)} %pad_clamp_fusion.1), kind=kCustom, calls=%fused_computation | custom fusion | bytes 4194312 | tf_op jit(solution)/shard_map/gather | solution.py:148
  28.1 1.3 collective-permute-start.2
  30.7 3.9 collective-permute-done.2
  34.6 145.5 %while.19 = (s32[]{:T(128)}, f32[4,512]{1,0:T(4,128)S(1)}, f32[3,4]{0,1:T(4,128)S(1)}, f32[8,4,4]{0,2,1:T(4,128)S(1)}, f32[8,4,3]{0,1,2:T(4,128)S(1)}, /*index=5...) while((s32[]{:T(128)}, f32[4,512]{1,0:T(4,128)S(1)}, ...), condition=%wide.region_12.13_spmd, body=%wide.region_6.12_spmd.sunk | while | flops 4151593472 | bytes 128433032 | solution.py:194
  39.9 2.4 fusion.150
  42.5 3.5 convolution_bitcast_fusion.7
  46.0 0.9 fusion.151
  47.7 4.5 %fusion.152 = f32[128,64,128]{2,0,1:T(8,128)S(1)} fusion(f32[128,64,1]{0,1,2:T(8,128)S(1)} %maximum_bitcast_fusion.12, f32[64,64,128]{2,1,0:T(8,128)S(1)} %slice_add_fusion.9), kind=kOutput, calls=%fused_computation.17.clone.1 | convolution fusion | flops 805306368 | bytes 6324224 | tf_op jit(solution)/shard_map/while/body/zyc,kz->kyc/dot_general | solution.py:71
  53.1 1.9 copy.121
  55.0 1.4 copy_multiply_fusion.5
  56.6 1.5 maximum_add_fusion.5
  65.4 3.6 fusion.146
  69.0 3.5 convolution_bitcast_fusion.6
  74.1 4.7 %fusion.148 = f32[128,64,128]{2,0,1:T(8,128)S(1)} fusion(f32[128,64,1]{0,1,2:T(8,128)S(1)} %maximum_bitcast_fusion.12, f32[64,64,128]{2,1,0:T(8,128)S(1)} %slice_add_fusion.8), kind=kOutput, calls=%fused_computation.15.clone.1 | convolution fusion | flops 805306368 | bytes 6324224 | tf_op jit(solution)/shard_map/while/body/zyc,kz->kyc/dot_general | solution.py:71
  79.7 1.2 copy.120
  80.9 1.4 copy_multiply_fusion.4
  82.5 1.5 maximum_add_fusion.4
  84.0 4.0 fusion.154
  88.6 3.2 add_divide_fusion.3
  93.2 2.2 fusion.156
  99.5 0.9 multiply_reduce_fusion.5
  103.8 1.2 fusion.158
  111.0 2.4 fusion.150
  113.6 3.5 convolution_bitcast_fusion.7
  118.8 4.5 %fusion.152 = f32[128,64,128]{2,0,1:T(8,128)S(1)} fusion(f32[128,64,1]{0,1,2:T(8,128)S(1)} %maximum_bitcast_fusion.12, f32[64,64,128]{2,1,0:T(8,128)S(1)} %slice_add_fusion.9), kind=kOutput, calls=%fused_computation.17.clone.1 | convolution fusion | flops 805306368 | bytes 6324224 | tf_op jit(solution)/shard_map/while/body/zyc,kz->kyc/dot_general | solution.py:71
  124.1 1.4 copy.121
  125.5 1.4 copy_multiply_fusion.5
  127.1 1.5 maximum_add_fusion.5
  136.0 3.6 fusion.146
  139.5 3.5 convolution_bitcast_fusion.6
  144.7 5.0 %fusion.148 = f32[128,64,128]{2,0,1:T(8,128)S(1)} fusion(f32[128,64,1]{0,1,2:T(8,128)S(1)} %maximum_bitcast_fusion.12, f32[64,64,128]{2,1,0:T(8,128)S(1)} %slice_add_fusion.8), kind=kOutput, calls=%fused_computation.15.clone.1 | convolution fusion | flops 805306368 | bytes 6324224 | tf_op jit(solution)/shard_map/while/body/zyc,kz->kyc/dot_general | solution.py:71
  150.5 1.2 copy.120
  151.7 1.4 copy_multiply_fusion.4
  153.3 1.5 maximum_add_fusion.4
  154.8 4.0 fusion.154
  159.4 3.2 add_divide_fusion.3
  164.0 2.2 fusion.156
  170.3 0.9 multiply_reduce_fusion.5
  174.6 1.2 fusion.158
  181.2 197.4 %all-to-all-start = ((f32[64,1,224]{2,1,0:T(1,128)}), f32[64,1,224]{2,1,0:T(1,128)S(1)}, u32[]{:S(2)}, u32[]{:S(2)}) async-start(f32[64,1,224]{2,1,0:T(1,128)} %broadcast_in_dim.37), calls=%async_computation | async-start | bytes 131072 | tf_op jit(solution)/shard_map/all_to_all | solution.py:25
  379.3 24.2 %all-to-all-done = f32[64,1,224]{2,1,0:T(1,128)S(1)} async-done(((f32[64,1,224]{2,1,0:T(1,128)}), f32[64,1,224]{2,1,0:T(1,128)S(1)}, u32[]{:S(2)}, u32[]{:S(2)}) %all-to-all-start) | async-done | bytes 57376 | tf_op jit(solution)/shard_map/all_to_all | solution.py:25
  (131 shorter events, 28.7 us)
Async XLA Ops:
  0.6 10.6 %collective-permute-start.3 = (s32[8,4]{0,1:T(4,128)}, s32[8,4]{0,1:T(4,128)S(1)}, u32[]{:S(2)}, u32[]{:S(2)}) collective-permute-start(s32[8,4]{0,1:T(4,128)} %param.6), channel_id=1, source_target_pairs={{1,0},{2,1},{3,2},{4,3},{5,4},{6,5},{7,6},{8,7},{9,8},{10,9},{11,1... | collective-permute-start | bytes 392 | tf_op jit(solution)/shard_map/ppermute | solution.py:20
  1.9 19.3 %collective-permute-start = (s32[8,4]{0,1:T(4,128)}, s32[8,4]{0,1:T(4,128)S(1)}, u32[]{:S(2)}, u32[]{:S(2)}) collective-permute-start(s32[8,4]{0,1:T(4,128)} %param.6), channel_id=1, source_target_pairs={{0,1},{1,2},{2,3},{3,4},{4,5},{5,6},{6,7},{7,8},{8,9},{9,10},{10,1... | collective-permute-start | bytes 392 | tf_op jit(solution)/shard_map/ppermute | solution.py:20
  5.0 6.2 %collective-permute-start.4 = (s32[1]{0:T(128)}, s32[1]{0:T(128)}, u32[]{:S(2)}, u32[]{:S(2)}) collective-permute-start(s32[1]{0:T(128)} %param.7), channel_id=1, source_target_pairs={{1,0},{2,1},{3,2},{4,3},{5,4},{6,5},{7,6},{8,7},{9,8},{10,9},{11,1... | collective-permute-start | bytes 20 | tf_op jit(solution)/shard_map/ppermute | solution.py:20
  6.3 14.9 %collective-permute-start.1 = (s32[1]{0:T(128)}, s32[1]{0:T(128)}, u32[]{:S(2)}, u32[]{:S(2)}) collective-permute-start(s32[1]{0:T(128)} %param.7), channel_id=1, source_target_pairs={{0,1},{1,2},{2,3},{3,4},{4,5},{5,6},{6,7},{7,8},{8,9},{9,10},{10,1... | collective-permute-start | bytes 20 | tf_op jit(solution)/shard_map/ppermute | solution.py:20
  18.0 12.7 %collective-permute-start.5 = (bf16[2,64,64,128]{3,2,1,0:T(8,128)(2,1)}, bf16[2,64,64,128]{3,2,1,0:T(8,128)(2,1)S(1)}, u32[]{:S(2)}, u32[]{:S(2)}) collective-permute-start(bf16[2,64,64,128]{3,2,1,0:T(8,128)(2,1)} %gather_fusion.1), channel_id=1, source_target_pairs={{0,1},{1,2},{2,3},{3,4},{4,5},{5,6},{6,7},{7,8},{8,9},{9,10},{10,1... | collective-permute-start | bytes 6291464 | tf_op jit(solution)/shard_map/ppermute | solution.py:20
  22.6 7.5 %copy-start.3 = (s32[8,4]{0,1:T(4,128)S(1)}, s32[8,4]{0,1:T(4,128)}, u32[]{:S(2)}) copy-start(s32[8,4]{0,1:T(4,128)} %param.6) | copy-start | bytes 388
  28.1 6.4 %collective-permute-start.2 = (bf16[2,64,64,128]{3,2,1,0:T(8,128)(2,1)}, bf16[2,64,64,128]{3,2,1,0:T(8,128)(2,1)}, u32[]{:S(2)}, u32[]{:S(2)}) collective-permute-start(bf16[2,64,64,128]{3,2,1,0:T(8,128)(2,1)} %gather_fusion), channel_id=1, source_target_pairs={{1,0},{2,1},{3,2},{4,3},{5,4},{6,5},{7,6},{8,7},{9,8},{10,9},{11,1... | collective-permute-start | bytes 6291464 | tf_op jit(solution)/shard_map/ppermute | solution.py:20
  35.5 7.0 %copy-start = (bf16[2,64,64,128]{3,2,1,0:T(8,128)(2,1)}, bf16[2,64,64,128]{3,2,1,0:T(8,128)(2,1)S(1)}, u32[]{:S(2)}) copy-start(bf16[2,64,64,128]{3,2,1,0:T(8,128)(2,1)S(1)} %get-tuple-element.577) | copy-start | bytes 6291460 | tf_op jit(solution)/shard_map/while
  95.4 10.0 %copy-start.1 = (bf16[2,64,64,128]{3,2,1,0:T(8,128)(2,1)S(1)}, bf16[2,64,64,128]{3,2,1,0:T(8,128)(2,1)}, u32[]{:S(2)}) copy-start(bf16[2,64,64,128]{3,2,1,0:T(8,128)(2,1)} %copy-done) | copy-start | bytes 6291460 | tf_op jit(solution)/shard_map/while
  106.5 7.0 %copy-start = (bf16[2,64,64,128]{3,2,1,0:T(8,128)(2,1)}, bf16[2,64,64,128]{3,2,1,0:T(8,128)(2,1)S(1)}, u32[]{:S(2)}) copy-start(bf16[2,64,64,128]{3,2,1,0:T(8,128)(2,1)S(1)} %get-tuple-element.577) | copy-start | bytes 6291460 | tf_op jit(solution)/shard_map/while
  166.2 10.0 %copy-start.1 = (bf16[2,64,64,128]{3,2,1,0:T(8,128)(2,1)S(1)}, bf16[2,64,64,128]{3,2,1,0:T(8,128)(2,1)}, u32[]{:S(2)}) copy-start(bf16[2,64,64,128]{3,2,1,0:T(8,128)(2,1)} %copy-done) | copy-start | bytes 6291460 | tf_op jit(solution)/shard_map/while
  180.1 225.1 %copy-start.2 = (f32[4,512]{1,0:T(4,128)}, f32[4,512]{1,0:T(4,128)S(1)}, u32[]{:S(2)}) copy-start(f32[4,512]{1,0:T(4,128)S(1)} %get-tuple-element.252) | copy-start | bytes 24580
  181.2 222.3 %all-to-all-start = ((f32[64,1,224]{2,1,0:T(1,128)}), f32[64,1,224]{2,1,0:T(1,128)S(1)}, u32[]{:S(2)}, u32[]{:S(2)}) async-start(f32[64,1,224]{2,1,0:T(1,128)} %broadcast_in_dim.37), calls=%async_computation | async-start | bytes 131072 | tf_op jit(solution)/shard_map/all_to_all | solution.py:25
where the time goes:
time: 411 us; the launch traced here: 406 us
  starting transfers between devices  213 us (52%)
  matrix products  51.5 us (13%)
  other arithmetic  46 us (11%)
  loops' own time  37.1 us (9%)
  local copies, waits for them, and re-layouts  28.6 us (7%)
  waiting for transfers between devices  28.1 us (7%)
    all_to_all x1, starting transfers between devices, sent_to_all(): lax.all_to_all(jnp.broadcast_to(shard[None], (devices, *shard.shape)), ax...  197 us
    another operation x1, loops' own time, on_device(): lax.fori_loop(jnp.int32(0), live_count, own_step, start_state)  37.1 us
    all_to_all x1, waiting for transfers between devices, sent_to_all(): lax.all_to_all(jnp.broadcast_to(shard[None], (devices, *shard.shape)), ax...  24.2 us
    dot_general x4, matrix products, spectrum(): mixed = jnp.einsum('zyc,kz->kyc', spectra, stacked, precision=PRECISE)  18.8 us
    ppermute x6, starting transfers between devices, passed_along(): lax.ppermute(value, axis, [(source, source + steps) for source in range(l...  15.1 us
    dot_general x4, matrix products, spectrum(): mixed = jnp.einsum('zyc,ky->zkc', spectra, stacked, precision=PRECISE)  14 us
    dot_general x4, matrix products, spectrum(): jnp.dot(flat_rows, dft_table, precision=PRECISE, preferred_element_type=j...  11.9 us
    gather x2, local copies, waits for them, and re-layouts, requested(): return volumes[view_pick]  11 us
  transfers between devices with their start and end apart: 7, of which 2 were waited for; matrix products, arithmetic and copies ran while one was open for 4% of the time, Pallas kernels for 0%

commit v1 on v0

v1 whole, which is shorter than its diff:
```python
import math

import jax
import jax.numpy as jnp
import numpy as np
from jax import lax
from jax.experimental import pallas as pl
from jax.experimental.pallas import tpu as pltpu
from jax.sharding import PartitionSpec as P

WIN = 8
EPSILON = 1e-06
SLOTS = 4
EDGE = 64
HALF = 32
LANES = 128
ROWS = 8
XCHUNK = 8
F32 = jnp.float32
BF16 = jnp.bfloat16


def passed_along(value, axis, steps):
    count = lax.axis_size(axis)
    leading, last = (max(0, -steps), min(count, count - steps))
    return lax.ppermute(value, axis, [(source, source + steps) for source in range(leading, last)])


def basis_np():
    t = np.arange(EDGE)[:, None]
    s = np.arange(EDGE)[None, :]
    k = np.where(s <= HALF, s, s - HALF)
    angle = 2.0 * np.pi * ((k * t) % EDGE) / EDGE
    return np.where(s <= HALF, np.cos(angle), np.sin(angle))


def split_np(table):
    high = table.astype(BF16)
    low = (table - high.astype(np.float64)).astype(BF16)
    return high, low


def x_tables_np():
    table = basis_np()
    table = np.concatenate([table, table], axis=0)
    cos_part, sin_part = table[:, :HALF], table[:, HALF:]
    out = []
    for first, second in ((cos_part, sin_part), (sin_part, cos_part)):
        full = np.zeros((2 * LANES, LANES))
        for half in range(2):
            rows = slice(half * LANES, (half + 1) * LANES)
            full[rows, half * HALF : (half + 1) * HALF] = first
            full[rows, 2 * HALF + half * HALF : 2 * HALF + (half + 1) * HALF] = second
        out.append(np.concatenate(split_np(full), axis=1))
    return np.stack(out)


def y_table_np():
    high, low = split_np(basis_np().T)
    return np.concatenate([high, high, low], axis=1)


def split(values):
    high = values.astype(BF16)
    low = (values - high.astype(F32)).astype(BF16)
    return high, low


def times(value, angle_64):
    return value * float(np.float32(angle_64))


def rotate(re, im, phase):
    phase %= EDGE
    if phase == 0:
        return re, im
    c = math.cos(2.0 * math.pi * phase / EDGE)
    s = math.sin(2.0 * math.pi * phase / EDGE)
    if phase == EDGE // 4:
        return im, -re
    return times(re, c) + times(im, s), times(im, c) - times(re, s)


def real_dft8(x):
    r = math.sqrt(0.5)
    a0, a1, a2, a3 = x[0] + x[4], x[1] + x[5], x[2] + x[6], x[3] + x[7]
    b0, b1, b2, b3 = x[0] - x[4], x[1] - x[5], x[2] - x[6], x[3] - x[7]
    e0, e1 = a0 + a2, a1 + a3
    u, v = times(b1 - b3, r), times(b1 + b3, r)
    re = [e0 + e1, b0 + u, a0 - a2, b0 - u, e0 - e1]
    im = [None, -(b2 + v), a3 - a1, b2 - v, None]
    return re, im


def complex_dft4(re, im):
    a0r, a0i, a1r, a1i = re[0] + re[2], im[0] + im[2], re[0] - re[2], im[0] - im[2]
    b0r, b0i, b1r, b1i = re[1] + re[3], im[1] + im[3], re[1] - re[3], im[1] - im[3]
    return (
        [a0r + b0r, a1r + b1i, a0r - b0r, a1r - b1i],
        [a0i + b0i, a1i - b1r, a0i - b0i, a1i + b1r],
    )


def complex_dft8(re, im):
    er, ei = complex_dft4(re[0::2], im[0::2])
    odr, odi = complex_dft4(re[1::2], im[1::2])
    out_r, out_i = [None] * 8, [None] * 8
    for k in range(4):
        tr, ti = rotate(odr[k], odi[k], 8 * k)
        out_r[k], out_i[k] = er[k] + tr, ei[k] + ti
        out_r[k + 4], out_i[k + 4] = er[k] - tr, ei[k] - ti
    return out_r, out_i


def z_stage(grid_ref, column_ref):
    def column(index, carry):
        held = column_ref.at[index % 2]
        row = pl.multiple_of((index // 2) * ROWS, ROWS)
        lane = pl.multiple_of((index % 2) * LANES, LANES)

        def at(z):
            return grid_ref.at[z, pl.ds(row, ROWS), pl.ds(lane, LANES)]

        for z0 in range(8):
            re, im = real_dft8([at(8 * z1 + z0)[...] for z1 in range(8)])
            for n in range(5):
                held[8 * n + z0] = re[n]
            for n in range(1, 4):
                held[8 * (n + 4) + z0] = im[n]

        def keep(k, re, im):
            k %= EDGE
            if k > HALF:
                k, im = EDGE - k, -im
            at(k)[...] = re
            if k not in (0, HALF):
                at(HALF + k)[...] = -im

        re, im = real_dft8([held[z0] for z0 in range(8)])
        for n in range(5):
            keep(8 * n, re[n], im[n])
        y = [held[32 + z0] for z0 in range(8)]
        for first in (0, 1):
            sign = -1.0 if first == 0 else 1.0
            tr, ti = [], []
            for z0 in range(4):
                pr, pi = rotate(y[z0], sign * y[z0 + 4], 4 * z0 * (1 + 2 * first))
                tr.append(pr)
                ti.append(pi)
            dr, di = complex_dft4(tr, ti)
            keep(4 + 8 * first, dr[0], di[0])
            keep(4 + 8 * (first + 2), dr[1], di[1])
        for k1 in (1, 2, 3):
            re = [held[8 * k1 + z0] for z0 in range(8)]
            im = [held[8 * (k1 + 4) + z0] for z0 in range(8)]
            turned = [rotate(re[z0], im[z0], z0 * k1) for z0 in range(8)]
            dr, di = complex_dft8([p[0] for p in turned], [p[1] for p in turned])
            for k2 in range(8):
                keep(k1 + 8 * k2, dr[k2], di[k2])
        return carry

    lax.fori_loop(0, 2 * EDGE // ROWS, column, 0)


def masked_tables(table_ref, starts):
    out = []
    row = lax.broadcasted_iota(jnp.int32, (2 * LANES, 2 * LANES), 0)
    for part in range(2):
        low = jnp.where(row < LANES, starts[2 * part], starts[2 * part + 1])
        cell = row % LANES
        keep = (cell >= low) & (cell < low + EDGE)
        table = jnp.where(keep, table_ref[part].astype(F32), 0.0)
        out.append(table.astype(BF16))
    return out


def xy_stages(block_refs, wait_chunk, starts, x_table_ref, y_table_ref, masked_ref, grid_ref):
    for part, table in enumerate(masked_tables(x_table_ref, starts)):
        masked_ref[part] = table
    lane = lax.broadcasted_iota(jnp.int32, (XCHUNK * EDGE, LANES), 1)
    low_half = lane < EDGE

    def x_chunk(chunk, carry):
        first = chunk * XCHUNK
        wait_chunk(chunk)
        halves = []
        for part in range(2):
            rows = [
                block_refs[2 * part + k][pl.ds(first, XCHUNK)].reshape(XCHUNK * EDGE, LANES)
                for k in range(2)
            ]
            both = jnp.dot(
                jnp.concatenate(rows, axis=1), masked_ref[part], preferred_element_type=F32
            )
            halves.append(both[:, :LANES] + both[:, LANES:])
        cos_part = jnp.where(low_half, halves[0], halves[1])
        sin_part = pltpu.roll(jnp.where(low_half, halves[1], halves[0]), EDGE, 1)
        grid_ref[pl.ds(first, XCHUNK), :, :LANES] = cos_part.reshape(XCHUNK, EDGE, LANES)
        grid_ref[pl.ds(first, XCHUNK), :, LANES:] = sin_part.reshape(XCHUNK, EDGE, LANES)
        return carry

    lax.fori_loop(0, EDGE // XCHUNK, x_chunk, 0)

    def y_step(step, carry):
        for k in range(4):
            z = step * 4 + k
            high, low = split(grid_ref[z])
            grid_ref[z] = jnp.dot(
                y_table_ref[...],
                jnp.concatenate([high, low, high], axis=0),
                preferred_element_type=F32,
            )
        return carry

    lax.fori_loop(0, EDGE // 4, y_step, 0)


def zy_forward(cc, cs, sc, ss, z_zero, row_zero):
    if z_zero:
        return cc, cs, sc, ss
    r1, i1, r2, i2 = cc - ss, sc + cs, cc + ss, sc - cs
    if row_zero is not None:
        r1, i1 = jnp.where(row_zero, cc, r1), jnp.where(row_zero, sc, i1)
        r2, i2 = jnp.where(row_zero, cs, r2), jnp.where(row_zero, ss, i2)
    return r1, i1, r2, i2


def zy_adjoint(r1, i1, r2, i2, z_zero, row_zero):
    if z_zero:
        return r1, i1, r2, i2
    cc, cs, sc, ss = r1 + r2, i1 - i2, i1 + i2, r2 - r1
    if row_zero is not None:
        cc, sc = jnp.where(row_zero, r1, cc), jnp.where(row_zero, i1, sc)
        cs, ss = jnp.where(row_zero, r2, cs), jnp.where(row_zero, i2, ss)
    return cc, cs, sc, ss


def x_forward(rp, ip, rq, iq, lane_zero, row_zero):
    fa, fc = jnp.where(lane_zero, rp, rp - iq), jnp.where(lane_zero, ip, ip + rq)
    fb, fd = jnp.where(lane_zero, rq, rp + iq), jnp.where(lane_zero, iq, rq - ip)
    if row_zero is not None:
        fa, fc = jnp.where(row_zero, rp, fa), jnp.where(row_zero, rq, fc)
        fb, fd = jnp.where(row_zero, ip, fb), jnp.where(row_zero, iq, fd)
    return (fa, fc), (fb, fd)


def x_adjoint(first, second, lane_zero, row_zero):
    (ga, gc), (gb, gd) = first, second
    rp, iq = jnp.where(lane_zero, ga, ga + gb), jnp.where(lane_zero, gd, gb - ga)
    ip, rq = jnp.where(lane_zero, gc, gc - gd), jnp.where(lane_zero, gb, gc + gd)
    if row_zero is not None:
        rp, rq = jnp.where(row_zero, ga, rp), jnp.where(row_zero, gc, rq)
        ip, iq = jnp.where(row_zero, gb, ip), jnp.where(row_zero, gd, iq)
    return rp, ip, rq, iq


def octet(ref, kz, tile):
    row = tile * ROWS
    return [
        [
            ref.at[kz + dz, row + dy : row + dy + ROWS, lane : lane + LANES]
            for dz in (0, HALF)
            for dy in (0, HALF)
        ]
        for lane in (0, LANES)
    ]


def four_frequencies(ref, kz, tile, z_zero, lane_zero, row_zero):
    edge_row = row_zero if tile == 0 else None
    sides = []
    for pieces in octet(ref, kz, tile):
        cc, cs, sc, ss = [piece[...] for piece in pieces]
        sides.append(zy_forward(cc, cs, sc, ss, z_zero, edge_row))
    (rp1, ip1, rp2, ip2), (rq1, iq1, rq2, iq2) = sides
    corner_row = edge_row if z_zero else None
    return [
        *x_forward(rp1, ip1, rq1, iq1, lane_zero, corner_row),
        *x_forward(rp2, ip2, rq2, iq2, lane_zero, corner_row),
    ]


def cross_pass(grid_a, grid_b, size_ref, lane_zero, row_zero):
    corner = lane_zero & row_zero

    def one(kz, z_zero, total):
        for tile in range(4):
            fa = four_frequencies(grid_a, kz, tile, z_zero, lane_zero, row_zero)
            fb = four_frequencies(grid_b, kz, tile, z_zero, lane_zero, row_zero)
            pieces = [piece for side in octet(grid_b, kz, tile) for piece in side]
            for n in range(4):
                (ar, ai), (br, bi) = fa[n], fb[n]
                rr, ii = ar * br, ai * bi
                cr, ci = rr + ii, ai * br - ar * bi
                if z_zero and tile == 0:
                    cr, ci = jnp.where(corner, rr, cr), jnp.where(corner, ii, ci)
                size = jnp.sqrt(cr * cr + ci * ci)
                counted = size
                if z_zero and tile == 0:
                    counted = jnp.where(corner, 0.5 * (jnp.abs(cr) + jnp.abs(ci)), size)
                total = total + counted
                pieces[2 * n][...] = cr
                pieces[2 * n + 1][...] = ci
                size_ref[kz, tile, n] = size
        return total

    total = one(0, True, jnp.zeros((ROWS, LANES), F32))
    return lax.fori_loop(1, HALF, lambda kz, total: one(kz, False, total), total)


def ratio_pass(grid_b, size_ref, floor, lane_zero, row_zero):
    corner = lane_zero & row_zero

    def one(kz, z_zero):
        for tile in range(4):
            sides = octet(grid_b, kz, tile)
            pieces = [piece for side in sides for piece in side]
            ratios = []
            for n in range(4):
                cr, ci = pieces[2 * n][...], pieces[2 * n + 1][...]
                inverse = 1.0 / (size_ref[kz, tile, n] + floor)
                gr, gi = cr * inverse, ci * inverse
                if z_zero and tile == 0:
                    gr = jnp.where(corner, 0.5 * cr / (jnp.abs(cr) + floor), gr)
                    gi = jnp.where(corner, 0.5 * ci / (jnp.abs(ci) + floor), gi)
                ratios.append((gr, gi))
            edge_row = row_zero if tile == 0 else None
            corner_row = edge_row if z_zero else None
            rp1, ip1, rq1, iq1 = x_adjoint(ratios[0], ratios[1], lane_zero, corner_row)
            rp2, ip2, rq2, iq2 = x_adjoint(ratios[2], ratios[3], lane_zero, corner_row)
            for side, parts in zip(sides, ((rp1, ip1, rp2, ip2), (rq1, iq1, rq2, iq2))):
                for piece, value in zip(side, zy_adjoint(*parts, z_zero, edge_row)):
                    piece[...] = value

    one(0, True)

    def step(kz, carry):
        one(kz, False)
        return carry

    lax.fori_loop(1, HALF, step, 0)


def window_sums(grid_b, vy_ref, vz_ref, vx_ref):
    group = lax.broadcasted_iota(jnp.int32, (ROWS, 2 * LANES), 1) % LANES // HALF

    def step(number, carry):
        sums = list(carry)
        for k in range(2):
            sz = number * 2 + k
            high, low = split(grid_b[sz])
            mixed = jnp.dot(
                vy_ref[...], jnp.concatenate([high, low, high], axis=0), preferred_element_type=F32
            )
            rows = mixed[: WIN]
            for p in range(1, SLOTS):
                rows = jnp.where(group == p, mixed[p * WIN : (p + 1) * WIN], rows)
            for i in range(WIN):
                weight = jnp.broadcast_to(vz_ref[sz, i : i + 1, :], (ROWS, LANES))
                sums[2 * i] = sums[2 * i] + rows[:, :LANES] * weight
                sums[2 * i + 1] = sums[2 * i + 1] + rows[:, LANES:] * weight
        return tuple(sums)

    zero = jnp.zeros((ROWS, LANES), F32)
    sums = lax.fori_loop(0, EDGE // 2, step, (zero,) * (2 * WIN))
    stacked = jnp.concatenate(
        [jnp.concatenate([sums[2 * i], sums[2 * i + 1]], axis=1) for i in range(WIN)], axis=0
    )
    high, low = split(stacked)
    return jnp.dot(
        jnp.concatenate([high, low, high], axis=1), vx_ref[...], preferred_element_type=F32
    )


def first_kernel(fields, volumes_ref, x_table_ref, y_table_ref, out_ref, blocks, column, masked, sems):
    chunks = EDGE // XCHUNK

    def copy(p, chunk):
        view = fields[0, p]
        return pltpu.make_async_copy(
            volumes_ref.at[view, pl.ds(chunk * XCHUNK, XCHUNK)],
            blocks.at[p, pl.ds(chunk * XCHUNK, XCHUNK)],
            sems.at[p, chunk],
        )

    for chunk in range(chunks):
        for p in range(SLOTS):
            copy(p, chunk).start()

    def wait_chunk(chunk):
        for p in range(SLOTS):
            copy(p, chunk).wait()

    starts = [fields[1, p] for p in range(SLOTS)]
    xy_stages(
        [blocks.at[p] for p in range(SLOTS)],
        wait_chunk,
        starts,
        x_table_ref,
        y_table_ref,
        masked,
        out_ref,
    )
    z_stage(out_ref, column)


def rank_of(fields, slot, direction):
    rank = jnp.int32(0)
    for earlier in range(slot):
        rank = rank + (fields[3, earlier] == direction).astype(jnp.int32)
    return jnp.minimum(rank, 1)


def second_kernel(
    fields,
    counts,
    place,
    volumes_ref,
    above_ref,
    below_ref,
    grid_a_hbm,
    x_table_ref,
    y_table_ref,
    vy_ref,
    vz_ref,
    vx_ref,
    corr_ref,
    shift_ref,
    part_ref,
    blocks,
    grid_a,
    grid_b,
    sizes,
    column,
    masked,
    sems,
    a_sem,
):
    chunks = EDGE // XCHUNK
    a_copy = pltpu.make_async_copy(grid_a_hbm, grid_a, a_sem)

    def copy_from(source, p, chunk):
        return pltpu.make_async_copy(
            source.at[pl.ds(chunk * XCHUNK, XCHUNK)],
            blocks.at[p, pl.ds(chunk * XCHUNK, XCHUNK)],
            sems.at[p, chunk],
        )

    for chunk in range(chunks):
        for p in range(SLOTS):
            side = fields[3, p]
            for value, source in ((0, volumes_ref.at[fields[2, p]]), (1, above_ref), (-1, below_ref)):

                @pl.when(side == value)
                def _(source=source):
                    copy_from(source, p, chunk).start()

    a_copy.start()

    def wait_chunk(chunk):
        for p in range(SLOTS):
            copy_from(above_ref, p, chunk).wait()

    starts = []
    for p in range(SLOTS):
        side = fields[3, p]
        starts.append(jnp.where(side == 0, fields[4, p], EDGE * rank_of(fields, p, side)))
    xy_stages(
        [blocks.at[p] for p in range(SLOTS)],
        wait_chunk,
        starts,
        x_table_ref,
        y_table_ref,
        masked,
        grid_b,
    )
    z_stage(grid_b, column)
    a_copy.wait()
    lane = lax.broadcasted_iota(jnp.int32, (ROWS, LANES), 1)
    row = lax.broadcasted_iota(jnp.int32, (ROWS, LANES), 0)
    lane_zero, row_zero = lane % HALF == 0, row == 0
    total = cross_pass(grid_a, grid_b, sizes, lane_zero, row_zero)
    floor = jnp.zeros((1, LANES), F32)
    for p in range(SLOTS):
        mine = lane // HALF == p
        whole = jnp.sum(jnp.where(mine, total, 0.0), axis=(0, 1), keepdims=True)
        floor = jnp.where(mine[:1], whole * (2.0 / EDGE**3) + EPSILON, floor)
    floor = jnp.broadcast_to(floor, (ROWS, LANES))
    ratio_pass(grid_b, sizes, floor, lane_zero, row_zero)
    values = window_sums(grid_b, vy_ref, vz_ref, vx_ref)
    corr_ref[...] = values
    weight = values * values
    at = lax.broadcasted_iota(jnp.int32, (WIN * WIN, LANES), 0)
    along = [(at // WIN).astype(F32), (at % WIN).astype(F32)]
    k_row = (lane[:1] % WIN).astype(F32)
    plain = jnp.sum(weight, axis=0, keepdims=True)
    sums = [plain] + [jnp.sum(weight * a, axis=0, keepdims=True) for a in along] + [plain * k_row]
    stats = jnp.concatenate(sums + [jnp.zeros((ROWS - 4, LANES), F32)], axis=0) * (1.0 / WIN**3)
    for amount in (1, 2, 4):
        stats = stats + pltpu.roll(stats, LANES - amount, 1)
    shift_out = jnp.zeros((ROWS, LANES), F32)
    part = jnp.zeros((ROWS, LANES), F32)
    normal_lane = lane < 16
    first_of = jnp.where(normal_lane, lane // 4, (lane - 16) // 3)
    second_of = jnp.where(normal_lane, lane % 4, (lane - 16) % 3)
    edge = float(EDGE)
    slab_height = (place[0].astype(F32) * edge + 0.5 * edge) / (edge * place[1].astype(F32))
    for p in range(SLOTS):
        energy = stats[0:1, p * WIN : p * WIN + 1]
        moved = []
        for axis in range(3):
            first_moment = stats[axis + 1 : axis + 2, p * WIN : p * WIN + 1]
            moment = first_moment + energy * fields[5 + axis, p].astype(F32)
            moved.append(moment / (energy + EPSILON))
        anchor = (fields[1, p].astype(F32) + 0.5 * edge) / (2.0 * edge)

        def center(index):
            last = jnp.where(index == 2, anchor, 1.0)
            return jnp.where(index == 0, slab_height, jnp.where(index == 1, 0.5, last))

        moved_lane = jnp.where(
            second_of == 0, moved[0], jnp.where(second_of == 1, moved[1], moved[2])
        )
        other = jnp.where(normal_lane, center(second_of), moved_lane)
        hit_a = (row == fields[0, p]).astype(F32)
        hit_b = (row == fields[2, p]).astype(F32)
        hits = jnp.where(normal_lane, hit_a + hit_b, hit_a - hit_b)
        part = part + hits * (energy * center(first_of) * other)
        for axis in range(3):
            shift_out = jnp.where((lane == p) & (row == axis), moved[axis], shift_out)
    shift_ref[...] = shift_out
    part_ref[...] = jnp.where(lane < 28, part, 0.0)


def pick_view(fields, direction, rank):
    view = jnp.int32(0)
    seen = jnp.int32(0)
    for slot in range(SLOTS):
        asked = fields[3, slot] == direction
        view = jnp.where(asked & (seen == rank), fields[2, slot], view)
        seen = seen + asked.astype(jnp.int32)
    return view


def pick_start(fields, direction, rank):
    start = jnp.int32(0)
    seen = jnp.int32(0)
    for slot in range(SLOTS):
        asked = fields[3, slot] == direction
        start = jnp.where(asked & (seen == rank), fields[4, slot], start)
        seen = seen + asked.astype(jnp.int32)
    return start


def pack_kernel(below, above, b0_ref, b1_ref, a0_ref, a1_ref, down_ref, up_ref):
    planes = b0_ref.shape[1]
    lane = lax.broadcasted_iota(jnp.int32, (EDGE, LANES), 1)
    cell = lane % EDGE
    for fields, direction, first_ref, second_ref, out_ref in (
        (below, 1, b0_ref, b1_ref, down_ref),
        (above, -1, a0_ref, a1_ref, up_ref),
    ):
        plain_first = cell >= pick_start(fields, direction, 0)
        plain_second = cell < pick_start(fields, direction, 1)
        low_half = lane < EDGE
        keep = jnp.where(low_half, plain_first.astype(F32), plain_second.astype(F32)) > 0.0
        for z in range(planes):
            chosen = jnp.where(low_half, first_ref[0, z].astype(F32), second_ref[0, z].astype(F32))
            crossed = jnp.where(low_half, second_ref[0, z].astype(F32), first_ref[0, z].astype(F32))
            out_ref[z] = jnp.where(keep, chosen, pltpu.roll(crossed, EDGE, 1)).astype(BF16)


def packed_blocks(volumes, below_fields, above_fields):
    planes = 16
    block = (1, planes, EDGE, LANES)

    def taken(from_below, rank):
        def index(i, below, above):
            fields, direction = (below, 1) if from_below else (above, -1)
            return pick_view(fields, direction, rank), i, 0, 0

        return pl.BlockSpec(block, index)

    out_block = pl.BlockSpec((planes, EDGE, LANES), lambda i, below, above: (i, 0, 0))
    shape = jax.ShapeDtypeStruct((EDGE, EDGE, LANES), BF16)
    return pl.pallas_call(
        pack_kernel,
        out_shape=(shape, shape),
        grid_spec=pltpu.PrefetchScalarGridSpec(
            num_scalar_prefetch=2,
            grid=(EDGE // planes,),
            in_specs=[taken(True, 0), taken(True, 1), taken(False, 0), taken(False, 1)],
            out_specs=(out_block, out_block),
        ),
        name="pack",
    )(below_fields, above_fields, volumes, volumes, volumes, volumes)


def first_spectra(volumes, pair_fields, x_tables, y_table):
    whole = pl.BlockSpec(memory_space=pltpu.VMEM)
    return pl.pallas_call(
        first_kernel,
        out_shape=jax.ShapeDtypeStruct((EDGE, EDGE, 2 * LANES), F32),
        in_specs=[
            pl.BlockSpec(memory_space=pltpu.SMEM),
            pl.BlockSpec(memory_space=pl.ANY),
            whole,
            whole,
        ],
        out_specs=whole,
        scratch_shapes=[
            pltpu.VMEM((SLOTS, EDGE, EDGE, LANES), BF16),
            pltpu.VMEM((2, EDGE, ROWS, LANES), F32),
            pltpu.VMEM((2, 2 * LANES, 2 * LANES), BF16),
            pltpu.SemaphoreType.DMA((SLOTS, EDGE // XCHUNK)),
        ],
        name="first_spectra",
    )(pair_fields, volumes, x_tables, y_table)


def correlated(volumes, above, below, grid_a, pair_fields, pair_counts, place, tables):
    whole = pl.BlockSpec(memory_space=pltpu.VMEM)
    scalar = pl.BlockSpec(memory_space=pltpu.SMEM)
    left = pl.BlockSpec(memory_space=pl.ANY)
    grid = pltpu.VMEM((EDGE, EDGE, 2 * LANES), F32)
    return pl.pallas_call(
        second_kernel,
        out_shape=(
            jax.ShapeDtypeStruct((WIN * WIN, LANES), F32),
            jax.ShapeDtypeStruct((ROWS, LANES), F32),
            jax.ShapeDtypeStruct((ROWS, LANES), F32),
        ),
        in_specs=[scalar] * 3 + [left] * 4 + [whole] * 5,
        out_specs=(whole,) * 3,
        scratch_shapes=[
            pltpu.VMEM((SLOTS, EDGE, EDGE, LANES), BF16),
            grid,
            grid,
            pltpu.VMEM((HALF, 4, 4, ROWS, LANES), F32),
            pltpu.VMEM((2, EDGE, ROWS, LANES), F32),
            pltpu.VMEM((2, 2 * LANES, 2 * LANES), BF16),
            pltpu.SemaphoreType.DMA((SLOTS, EDGE // XCHUNK)),
            pltpu.SemaphoreType.DMA,
        ],
        name="correlated",
    )(pair_fields, pair_counts, place, volumes, above, below, grid_a, *tables)


def split_outside(values):
    high = lax.reduce_precision(values, 8, 7)
    return high.astype(BF16), (values - high).astype(BF16)


def window_tables(pair_fields, pair_counts):
    slot = jnp.arange(EDGE, dtype=jnp.int32)
    freq = jnp.where(slot <= HALF, slot, slot - HALF)
    steps = jnp.arange(WIN, dtype=jnp.int32)
    offsets = pair_fields[5:8] + jnp.array([[0], [0], [1]], jnp.int32) * (
        pair_fields[1] - pair_fields[4]
    )
    where_at = offsets[:, :, None, None] + steps[None, None, :, None]
    phase = jnp.mod(where_at * freq, EDGE) - jnp.where(slot <= HALF, 0, EDGE // 4)
    values = jnp.cos((2.0 * math.pi / EDGE) * phase.astype(F32))
    vz = jnp.repeat(jnp.transpose(values[0], (2, 1, 0)), HALF, axis=2)
    high, low = split_outside(values[1].reshape(SLOTS * WIN, EDGE))
    vy = jnp.concatenate([high, high, low], axis=1)
    live = (jnp.arange(SLOTS) < pair_counts[0]).astype(F32) * (2.0 / EDGE**1.5)
    vx = values[2] * live[:, None, None]
    vx = jnp.transpose(vx.reshape(SLOTS, WIN, 2, HALF), (2, 0, 3, 1))
    own = jnp.eye(SLOTS, dtype=F32)
    vx = (vx[:, :, :, None, :] * own[None, :, None, :, None]).reshape(2 * LANES, SLOTS * WIN)
    vx = jnp.pad(vx, ((0, 0), (0, LANES - SLOTS * WIN)))
    high, low = split_outside(vx)
    return vy, vz, jnp.concatenate([high, high, low], axis=0)


def group_sum(part, axis, size, stride):
    count = lax.axis_size(axis)
    groups = [
        [base + first + stride * k for k in range(size)]
        for base in range(0, count, size * stride)
        for first in range(stride)
    ]
    every = lax.all_gather(part, axis, axis=0, tiled=False, axis_index_groups=groups)
    return jnp.sum(every, axis=0)


def on_device(volumes, pair_fields, pair_counts):
    view_count = volumes.shape[0]
    slab_count = lax.axis_size("slab")
    own_index = lax.axis_index("slab")
    below_fields = passed_along(pair_fields, "slab", 1)
    above_fields = passed_along(pair_fields, "slab", -1)
    down, up = packed_blocks(volumes, below_fields, above_fields)
    from_above = passed_along(down, "slab", -1)
    from_below = passed_along(up, "slab", 1)
    x_tables, y_table = jnp.asarray(x_tables_np()), jnp.asarray(y_table_np())
    grid_a = first_spectra(volumes, pair_fields, x_tables, y_table)
    vy, vz, vx = window_tables(pair_fields, pair_counts)
    place = jnp.stack([own_index.astype(jnp.int32), jnp.int32(slab_count)])
    corr, shift, part = correlated(
        volumes,
        from_above,
        from_below,
        grid_a,
        pair_fields,
        pair_counts,
        place,
        (x_tables, y_table, vy, vz, vx),
    )
    corr = jnp.transpose(corr[:, : SLOTS * WIN].reshape(WIN * WIN, SLOTS, WIN), (1, 0, 2))
    corr = corr.reshape(SLOTS, WIN**3)
    first = 1
    while 2 * first * first <= slab_count:
        first *= 2
    while slab_count % first:
        first -= 1
    part = group_sum(part, "slab", first, 1)
    part = group_sum(part, "slab", slab_count // first, first)
    part = part * (1.0 / (SLOTS * slab_count))
    normal = part[:view_count, :16].reshape(view_count, 4, 4)
    rhs = part[:view_count, 16:28].reshape(view_count, 4, 3)
    return corr, shift[:3, :SLOTS], normal, rhs


def solution(mesh):
    in_specs = (P("tm", "slab", None, None), P(None, ("tm", "slab")), P(("tm", "slab")))
    out_specs = (
        P(("tm", "slab"), None),
        P(None, ("tm", "slab")),
        P("tm", None, None),
        P("tm", None, None),
    )
    return jax.shard_map(
        on_device, mesh=mesh, in_specs=in_specs, out_specs=out_specs, check_vma=False
    )
```

time: 411 us -> 137 us (0.33); the launches traced: 406 us -> 136 us
  starting transfers between devices: 213 us -> 9.5 us
  blocking collectives: 0 us -> 73.1 us
  matrix products: 51.5 us -> 0 us
  other arithmetic: 46 us -> 4.3 us
  Pallas kernels: 0 us -> 38 us
  loops' own time: 37.1 us -> 0 us
  waiting for transfers between devices: 28.1 us -> 0.01 us
  local copies, waits for them, and re-layouts: 28.6 us -> 9.67 us
    all_to_all x1 -> x0, starting transfers between devices: 197 us -> none  [sent_to_all(): lax.all_to_all(jnp.broadcast_to(shard[None], (devices, *shard.shape)), ax...]
    all_gather x0 -> x2, blocking collectives: none -> 73.1 us  [group_sum(): lax.all_gather(part, axis, axis=0, tiled=False, axis_index_groups=groups)]
    dot_general x18 -> x0, matrix products: 51.5 us -> none  [the longest x4 18.8 us: spectrum(): mixed = jnp.einsum('zyc,kz->kyc', spectra, stacked, precision=PRECISE)]
    pallas_call x0 -> x3, Pallas kernels: none -> 38 us  [the longest x1 20 us: correlated(): pl.pallas_call(second_kernel, out_shape=(jax.ShapeDtypeStruct((WIN * WIN,...]
    another operation x1 -> x0, loops' own time: 37.1 us -> none  [on_device(): lax.fori_loop(jnp.int32(0), live_count, own_step, start_state)]
    all_to_all x1 -> x0, waiting for transfers between devices: 24.2 us -> none  [sent_to_all(): lax.all_to_all(jnp.broadcast_to(shard[None], (devices, *shard.shape)), ax...]
    add x24 -> x2, other arithmetic: 13.6 us -> 0.83 us  [the longest x1 0.76 us: window_tables(): pair_fields[5:8]]
    gather x2 -> x0, local copies, waits for them, and re-layouts: 11 us -> none  [requested(): return volumes[view_pick]]
  transfers between devices with their start and end apart: 7 -> 4, of which waited for: 2 -> 0; matrix products, arithmetic and copies ran while one was open for 4% -> 4% of each run, Pallas kernels for 0% -> 9%
where the time goes in v1:
time: 137 us; the launch traced here: 136 us
  blocking collectives  73.1 us (53%)
  Pallas kernels  38 us (28%)
  local copies, waits for them, and re-layouts  9.67 us (7%)
  starting transfers between devices  9.5 us (7%)
  other arithmetic  4.3 us (3%)
  between operations  1.45 us (1%)
    all_gather x2, blocking collectives, group_sum(): lax.all_gather(part, axis, axis=0, tiled=False, axis_index_groups=groups)  73.1 us
    pallas_call x1, Pallas kernels, correlated(): pl.pallas_call(second_kernel, out_shape=(jax.ShapeDtypeStruct((WIN * WIN,...  20 us
    pallas_call x1, Pallas kernels, first_spectra(): pl.pallas_call(first_kernel, out_shape=jax.ShapeDtypeStruct((EDGE, EDGE,...  12.1 us
    ppermute x4, starting transfers between devices, passed_along(): lax.ppermute(value, axis, [(source, source + steps) for source in range(l...  9.5 us
    pallas_call x1, Pallas kernels, packed_blocks(): pl.pallas_call(pack_kernel, out_shape=(shape, shape), grid_spec=pltpu.Pre...  5.89 us
    unnamed x12, local copies, waits for them, and re-layouts  4.59 us
  transfers between devices with their start and end apart: 4, of which 0 were waited for; matrix products, arithmetic and copies ran while one was open for 4% of the time, Pallas kernels for 9%

profile of v1, /device:TPU:38, one launch (start us, length us, event | category | flops | bytes accessed | tf_op | source)
XLA Modules:
  0.0 136.0 jit_solution(15389223883510084475)
XLA Ops:
  0.6 0.8 copy.67.fields
  1.4 0.0 copy-start.2
  1.4 1.3 collective-permute-start.1
  2.7 3.1 %collective-permute-start = (s32[8,4]{1,0:T(8,128)S(1)}, s32[8,4]{1,0:T(8,128)S(1)}, u32[]{:S(2)}, u32[]{:S(2)}) collective-permute-start(s32[8,4]{1,0:T(8,128)S(1)} %copy.67.fields), channel_id=1, source_target_pairs={{0,1},{1,2},{2,3},{3,4},{4,5},{5,6},{6,7},{7,8},{8,9},{9,10},{10,1... | collective-permute-start | bytes 392 | tf_op jit(solution)/shard_map/ppermute | solution.py:26
  5.8 0.9 subtract_reduce_fusion
  7.4 0.8 multiply_add_fusion
  8.2 0.1 copy.62
  8.2 0.1 iota_add_fusion
  8.3 0.3 fusion.4
  8.6 0.1 squeeze.12
  8.7 0.0 collective-permute-done.1.above
  8.7 0.0 copy-start.3
  8.7 0.0 collective-permute-done.below
  8.7 0.6 copy-done.3
  9.3 0.0 copy-start.4
  9.3 0.6 copy-done.4
  9.9 5.9 %pack.1 = (bf16[64,64,128]{2,1,0:T(8,128)(2,1)}, bf16[64,64,128]{2,1,0:T(8,128)(2,1)}) custom-call(s32[8,4]{1,0:T(8,128)} %copy-done.4, s32[8,4]{1,0:T(8,128)} %copy-done.3, bf16[8,64,64,128]{3,2,1,0:T(8,128)(2,1)} %volumes_ref.3, bf16[8,64,64,128]{3,2,1,0:T(8,128)(2,1)} %volumes_ref.3, bf16[8,64,64,128]{3,2,1,0:T(8,128)(2,1)} %volumes_ref.3, ...), custom_call_target="tpu_custom_call" | custom-call | tf_op jit(solution)/shard_map/pack/pallas_call | solution.py:586
  15.8 0.0 copy-done.2
  15.8 1.3 collective-permute-start.2
  17.1 3.8 %collective-permute-start.3 = (bf16[64,64,128]{2,1,0:T(8,128)(2,1)}, bf16[64,64,128]{2,1,0:T(8,128)(2,1)S(1)}, u32[]{:S(2)}, u32[]{:S(2)}) collective-permute-start(bf16[64,64,128]{2,1,0:T(8,128)(2,1)} %get-tuple-element.10), channel_id=1, source_target_pairs={{0,1},{1,2},{2,3},{3,4},{4,5},{5,6},{6,7},{7,8},{8,9},{9,10},{10,1... | collective-permute-start | bytes 3145736 | tf_op jit(solution)/shard_map/ppermute | solution.py:26
  20.9 0.1 fusion.6
  21.1 0.1 broadcast_multiply_fusion
  21.2 0.1 mul.87
  21.3 0.1 copy.66
  21.4 0.9 copy.68.vz_ref
  22.3 12.1 %first_spectra.1.grid_a_hbm = f32[64,64,256]{2,1,0:T(8,128)} custom-call(s32[8,4]{1,0:T(8,128)} %copy-done.2, bf16[8,64,64,128]{3,2,1,0:T(8,128)(2,1)} %volumes_ref.3, bf16[2,256,256]{2,1,0:T(8,128)(2,1)} %constant.43.clone.x_table_ref, bf16[64,192]{1,0:T(8,128)(2,1)} %constant.44.clone.y_table_ref), custom_call_target="tpu_custom_call" | custom-call | tf_op jit(solution)/shard_map/first_spectra/pallas_call | solution.py:601
  34.4 0.7 pad_add_fusion.place
  35.1 0.7 pad_maximum_fusion.1.vy_ref
  35.8 0.7 pad_maximum_fusion.vx_ref
  36.5 0.0 collective-permute-done.2.above_ref
  36.5 0.0 copy-start
  36.5 0.0 collective-permute-done.3.below_ref
  36.5 1.0 copy-done
  37.5 0.0 copy-start.1
  37.5 1.0 copy-done.1
  38.5 20.0 %correlated.1 = (f32[64,128]{1,0:T(8,128)}, f32[8,128]{1,0:T(8,128)}, f32[8,128]{1,0:T(8,128)}) custom-call(s32[8,4]{1,0:T(8,128)} %copy-done.2, s32[1]{0:T(128)} %copy.79.counts, s32[2]{0:T(128)} %pad_add_fusion.place, bf16[8,64,64,128]{3,2,1,0:T(8,128)(2,1)} %volumes_ref.3, bf16[64,64,128]{2,1,0:T(8,128)(2,1)} %copy-done, bf16[64,64,128]{2,1,0:T(8,128)(2,1)} %copy-done.1, ...), custom_call_target="tpu_custom_call" | custom-call | tf_op jit(solution)/shard_map/correlated/pallas_call | solution.py:626
  58.5 0.8 copy.69
  59.3 1.3 slice.37
  60.6 19.8 %all-gather = f32[64,128]{1,0:T(8,128)S(1)} all-gather(f32[8,128]{1,0:T(8,128)} %get-tuple-element.13), channel_id=2, replica_groups={{0,1,2,3,4,5,6,7},{8,9,10,11,12,13,14,15},{16,17,18,19,20,21,22,23},{24..., dimensions={0}, use_global_device_ids=true | all-gather | bytes 36864 | tf_op jit(solution)/shard_map/all_gather | solution.py:684
  80.3 53.3 %all-gather.1 = f32[64,128]{1,0:T(8,128)S(1)} all-gather(f32[8,128]{1,0:T(8,128)S(1)} %bitcast_reduce_fusion.1), channel_id=3, replica_groups={{0,8,16,24,32,40,48,56},{1,9,17,25,33,41,49,57},{2,10,18,26,34,42,50,58..., dimensions={0}, use_global_device_ids=true | all-gather | bytes 36864 | tf_op jit(solution)/shard_map/all_gather | solution.py:684
  133.7 0.1 slice.39
  133.7 0.7 copy.71
  134.4 0.1 reshape.69
  134.5 0.7 copy.73
  135.2 0.1 copy.70
  135.3 0.7 reshape.64
  (12 shorter events, 0.1 us)
Async XLA Ops:
  1.4 14.4 %copy-start.2 = (s32[8,4]{1,0:T(8,128)}, s32[8,4]{1,0:T(8,128)S(1)}, u32[]{:S(2)}) copy-start(s32[8,4]{1,0:T(8,128)S(1)} %copy.67.fields) | copy-start | bytes 388
  1.4 7.3 %collective-permute-start.1 = (s32[8,4]{1,0:T(8,128)S(1)}, s32[8,4]{1,0:T(8,128)S(1)}, u32[]{:S(2)}, u32[]{:S(2)}) collective-permute-start(s32[8,4]{1,0:T(8,128)S(1)} %copy.67.fields), channel_id=1, source_target_pairs={{1,0},{2,1},{3,2},{4,3},{5,4},{6,5},{7,6},{8,7},{9,8},{10,9},{11,1... | collective-permute-start | bytes 392 | tf_op jit(solution)/shard_map/ppermute | solution.py:26
  2.7 6.0 %collective-permute-start = (s32[8,4]{1,0:T(8,128)S(1)}, s32[8,4]{1,0:T(8,128)S(1)}, u32[]{:S(2)}, u32[]{:S(2)}) collective-permute-start(s32[8,4]{1,0:T(8,128)S(1)} %copy.67.fields), channel_id=1, source_target_pairs={{0,1},{1,2},{2,3},{3,4},{4,5},{5,6},{6,7},{7,8},{8,9},{9,10},{10,1... | collective-permute-start | bytes 392 | tf_op jit(solution)/shard_map/ppermute | solution.py:26
  8.7 0.6 copy-start.3
  9.3 0.6 copy-start.4
  15.8 20.7 %collective-permute-start.2 = (bf16[64,64,128]{2,1,0:T(8,128)(2,1)}, bf16[64,64,128]{2,1,0:T(8,128)(2,1)S(1)}, u32[]{:S(2)}, u32[]{:S(2)}) collective-permute-start(bf16[64,64,128]{2,1,0:T(8,128)(2,1)} %get-tuple-element.9), channel_id=1, source_target_pairs={{1,0},{2,1},{3,2},{4,3},{5,4},{6,5},{7,6},{8,7},{9,8},{10,9},{11,1... | collective-permute-start | bytes 3145736 | tf_op jit(solution)/shard_map/ppermute | solution.py:26
  17.1 19.4 %collective-permute-start.3 = (bf16[64,64,128]{2,1,0:T(8,128)(2,1)}, bf16[64,64,128]{2,1,0:T(8,128)(2,1)S(1)}, u32[]{:S(2)}, u32[]{:S(2)}) collective-permute-start(bf16[64,64,128]{2,1,0:T(8,128)(2,1)} %get-tuple-element.10), channel_id=1, source_target_pairs={{0,1},{1,2},{2,3},{3,4},{4,5},{5,6},{6,7},{7,8},{8,9},{9,10},{10,1... | collective-permute-start | bytes 3145736 | tf_op jit(solution)/shard_map/ppermute | solution.py:26
  36.5 1.0 copy-start
  37.5 1.0 copy-start.1

commit v2 on v1

--- a/solution.py
+++ b/solution.py
@@ -15,7 +15,11 @@
 HALF = 32
 LANES = 128
 ROWS = 8
-XCHUNK = 8
+XCHUNK = 16
+Y_UNROLL = 8
+W_UNROLL = 8
+PCHUNK = 8
+GRANT = 24 << 20
 F32 = jnp.float32
 BF16 = jnp.bfloat16
 
@@ -57,7 +61,8 @@
 
 def y_table_np():
     high, low = split_np(basis_np().T)
-    return np.concatenate([high, high, low], axis=1)
+    above = np.concatenate([high, high], axis=1)
+    return np.concatenate([above, np.concatenate([low, np.zeros_like(low)], axis=1)], axis=0)
 
 
 def split(values):
@@ -202,17 +207,16 @@
     lax.fori_loop(0, EDGE // XCHUNK, x_chunk, 0)
 
     def y_step(step, carry):
-        for k in range(4):
-            z = step * 4 + k
+        for k in range(Y_UNROLL):
+            z = step * Y_UNROLL + k
             high, low = split(grid_ref[z])
-            grid_ref[z] = jnp.dot(
-                y_table_ref[...],
-                jnp.concatenate([high, low, high], axis=0),
-                preferred_element_type=F32,
+            both = jnp.dot(
+                y_table_ref[...], jnp.concatenate([high, low], axis=0), preferred_element_type=F32
             )
+            grid_ref[z] = both[:EDGE] + both[EDGE:]
         return carry
 
-    lax.fori_loop(0, EDGE // 4, y_step, 0)
+    lax.fori_loop(0, EDGE // Y_UNROLL, y_step, 0)
 
 
 def zy_forward(cc, cs, sc, ss, z_zero, row_zero):
@@ -346,12 +350,13 @@
 
     def step(number, carry):
         sums = list(carry)
-        for k in range(2):
-            sz = number * 2 + k
+        for k in range(W_UNROLL):
+            sz = number * W_UNROLL + k
             high, low = split(grid_b[sz])
-            mixed = jnp.dot(
-                vy_ref[...], jnp.concatenate([high, low, high], axis=0), preferred_element_type=F32
+            both = jnp.dot(
+                vy_ref[...], jnp.concatenate([high, low], axis=0), preferred_element_type=F32
             )
+            mixed = both[: SLOTS * WIN] + both[SLOTS * WIN :]
             rows = mixed[: WIN]
             for p in range(1, SLOTS):
                 rows = jnp.where(group == p, mixed[p * WIN : (p + 1) * WIN], rows)
@@ -362,7 +367,7 @@
         return tuple(sums)
 
     zero = jnp.zeros((ROWS, LANES), F32)
-    sums = lax.fori_loop(0, EDGE // 2, step, (zero,) * (2 * WIN))
+    sums = lax.fori_loop(0, EDGE // W_UNROLL, step, (zero,) * (2 * WIN))
     stacked = jnp.concatenate(
         [jnp.concatenate([sums[2 * i], sums[2 * i + 1]], axis=1) for i in range(WIN)], axis=0
     )
@@ -372,11 +377,35 @@
     )
 
 
+def flattened(values, flat_ref):
+    rows, cols = WIN * WIN, WIN**3
+    parts, left = [], values[:, : SLOTS * WIN]
+    for _ in range(3):
+        part = left.astype(BF16)
+        parts.append(part)
+        left = left - part.astype(F32)
+    pair = lax.broadcasted_iota(jnp.int32, (rows, SLOTS * WIN), 1) // WIN
+    own = lax.broadcasted_iota(jnp.int32, (rows, cols), 0)
+    cell = lax.broadcasted_iota(jnp.int32, (rows, cols), 1) // WIN
+    for p in range(SLOTS):
+        mine = [jnp.where(pair == p, part.astype(F32), 0.0).astype(BF16) for part in parts]
+        spread = jnp.dot(
+            jnp.concatenate(mine, axis=1), flat_ref[...], preferred_element_type=F32
+        )
+        yield jnp.sum(jnp.where(own == cell, spread, 0.0), axis=0, keepdims=True)
+
+
+def flat_table_np():
+    row = np.arange(SLOTS * WIN)[:, None] % WIN
+    col = np.arange(WIN**3)[None, :] % WIN
+    return np.tile((row == col).astype(BF16), (3, 1))
+
+
 def first_kernel(fields, volumes_ref, x_table_ref, y_table_ref, out_ref, blocks, column, masked, sems):
     chunks = EDGE // XCHUNK
 
     def copy(p, chunk):
-        view = fields[0, p]
+        view = fields[p, 0]
         return pltpu.make_async_copy(
             volumes_ref.at[view, pl.ds(chunk * XCHUNK, XCHUNK)],
             blocks.at[p, pl.ds(chunk * XCHUNK, XCHUNK)],
@@ -391,7 +420,7 @@
         for p in range(SLOTS):
             copy(p, chunk).wait()
 
-    starts = [fields[1, p] for p in range(SLOTS)]
+    starts = [fields[p, 1] for p in range(SLOTS)]
     xy_stages(
         [blocks.at[p] for p in range(SLOTS)],
         wait_chunk,
@@ -407,37 +436,33 @@
 def rank_of(fields, slot, direction):
     rank = jnp.int32(0)
     for earlier in range(slot):
-        rank = rank + (fields[3, earlier] == direction).astype(jnp.int32)
+        rank = rank + (fields[earlier, 3] == direction).astype(jnp.int32)
     return jnp.minimum(rank, 1)
 
 
 def second_kernel(
     fields,
-    counts,
-    place,
     volumes_ref,
     above_ref,
     below_ref,
-    grid_a_hbm,
+    grid_a,
     x_table_ref,
     y_table_ref,
     vy_ref,
     vz_ref,
     vx_ref,
+    flat_ref,
     corr_ref,
     shift_ref,
     part_ref,
     blocks,
-    grid_a,
     grid_b,
     sizes,
     column,
     masked,
     sems,
-    a_sem,
 ):
     chunks = EDGE // XCHUNK
-    a_copy = pltpu.make_async_copy(grid_a_hbm, grid_a, a_sem)
 
     def copy_from(source, p, chunk):
         return pltpu.make_async_copy(
@@ -448,23 +473,21 @@
 
     for chunk in range(chunks):
         for p in range(SLOTS):
-            side = fields[3, p]
-            for value, source in ((0, volumes_ref.at[fields[2, p]]), (1, above_ref), (-1, below_ref)):
+            side = fields[p, 3]
+            for value, source in ((0, volumes_ref.at[fields[p, 2]]), (1, above_ref), (-1, below_ref)):
 
                 @pl.when(side == value)
                 def _(source=source):
                     copy_from(source, p, chunk).start()
 
-    a_copy.start()
-
     def wait_chunk(chunk):
         for p in range(SLOTS):
             copy_from(above_ref, p, chunk).wait()
 
     starts = []
     for p in range(SLOTS):
-        side = fields[3, p]
-        starts.append(jnp.where(side == 0, fields[4, p], EDGE * rank_of(fields, p, side)))
+        side = fields[p, 3]
+        starts.append(jnp.where(side == 0, fields[p, 4], EDGE * rank_of(fields, p, side)))
     xy_stages(
         [blocks.at[p] for p in range(SLOTS)],
         wait_chunk,
@@ -475,7 +498,6 @@
         grid_b,
     )
     z_stage(grid_b, column)
-    a_copy.wait()
     lane = lax.broadcasted_iota(jnp.int32, (ROWS, LANES), 1)
     row = lax.broadcasted_iota(jnp.int32, (ROWS, LANES), 0)
     lane_zero, row_zero = lane % HALF == 0, row == 0
@@ -488,7 +510,8 @@
     floor = jnp.broadcast_to(floor, (ROWS, LANES))
     ratio_pass(grid_b, sizes, floor, lane_zero, row_zero)
     values = window_sums(grid_b, vy_ref, vz_ref, vx_ref)
-    corr_ref[...] = values
+    for p, line in enumerate(flattened(values, flat_ref)):
+        corr_ref[p : p + 1, :] = line
     weight = values * values
     at = lax.broadcasted_iota(jnp.int32, (WIN * WIN, LANES), 0)
     along = [(at // WIN).astype(F32), (at % WIN).astype(F32)]
@@ -501,18 +524,19 @@
     shift_out = jnp.zeros((ROWS, LANES), F32)
     part = jnp.zeros((ROWS, LANES), F32)
     normal_lane = lane < 16
-    first_of = jnp.where(normal_lane, lane // 4, (lane - 16) // 3)
-    second_of = jnp.where(normal_lane, lane % 4, (lane - 16) % 3)
+    first_of = jnp.where(normal_lane, lane // 4, lane % 4)
+    second_of = jnp.where(normal_lane, lane % 4, (lane - 16) // 4)
     edge = float(EDGE)
-    slab_height = (place[0].astype(F32) * edge + 0.5 * edge) / (edge * place[1].astype(F32))
+    slab = lax.axis_index("slab").astype(F32)
+    slab_height = (slab * edge + 0.5 * edge) / (edge * lax.axis_size("slab"))
     for p in range(SLOTS):
         energy = stats[0:1, p * WIN : p * WIN + 1]
         moved = []
         for axis in range(3):
             first_moment = stats[axis + 1 : axis + 2, p * WIN : p * WIN + 1]
-            moment = first_moment + energy * fields[5 + axis, p].astype(F32)
+            moment = first_moment + energy * fields[p, 5 + axis].astype(F32)
             moved.append(moment / (energy + EPSILON))
-        anchor = (fields[1, p].astype(F32) + 0.5 * edge) / (2.0 * edge)
+        anchor = (fields[p, 1].astype(F32) + 0.5 * edge) / (2.0 * edge)
 
         def center(index):
             last = jnp.where(index == 2, anchor, 1.0)
@@ -522,13 +546,13 @@
             second_of == 0, moved[0], jnp.where(second_of == 1, moved[1], moved[2])
         )
         other = jnp.where(normal_lane, center(second_of), moved_lane)
-        hit_a = (row == fields[0, p]).astype(F32)
-        hit_b = (row == fields[2, p]).astype(F32)
+        hit_a = (row == fields[p, 0]).astype(F32)
+        hit_b = (row == fields[p, 2]).astype(F32)
         hits = jnp.where(normal_lane, hit_a + hit_b, hit_a - hit_b)
         part = part + hits * (energy * center(first_of) * other)
         for axis in range(3):
             shift_out = jnp.where((lane == p) & (row == axis), moved[axis], shift_out)
-    shift_ref[...] = shift_out
+    shift_ref[...] = shift_out[:3, :SLOTS]
     part_ref[...] = jnp.where(lane < 28, part, 0.0)
 
 
@@ -536,8 +560,8 @@
     view = jnp.int32(0)
     seen = jnp.int32(0)
     for slot in range(SLOTS):
-        asked = fields[3, slot] == direction
-        view = jnp.where(asked & (seen == rank), fields[2, slot], view)
+        asked = fields[slot, 3] == direction
+        view = jnp.where(asked & (seen == rank), fields[slot, 2], view)
         seen = seen + asked.astype(jnp.int32)
     return view
 
@@ -546,61 +570,82 @@
     start = jnp.int32(0)
     seen = jnp.int32(0)
     for slot in range(SLOTS):
-        asked = fields[3, slot] == direction
-        start = jnp.where(asked & (seen == rank), fields[4, slot], start)
+        asked = fields[slot, 3] == direction
+        start = jnp.where(asked & (seen == rank), fields[slot, 4], start)
         seen = seen + asked.astype(jnp.int32)
     return start
 
 
-def pack_kernel(below, above, b0_ref, b1_ref, a0_ref, a1_ref, down_ref, up_ref):
-    planes = b0_ref.shape[1]
+def pack_kernel(below, above, volumes_ref, down_ref, up_ref, held, sems):
     lane = lax.broadcasted_iota(jnp.int32, (EDGE, LANES), 1)
-    cell = lane % EDGE
-    for fields, direction, first_ref, second_ref, out_ref in (
-        (below, 1, b0_ref, b1_ref, down_ref),
-        (above, -1, a0_ref, a1_ref, up_ref),
-    ):
-        plain_first = cell >= pick_start(fields, direction, 0)
-        plain_second = cell < pick_start(fields, direction, 1)
-        low_half = lane < EDGE
-        keep = jnp.where(low_half, plain_first.astype(F32), plain_second.astype(F32)) > 0.0
-        for z in range(planes):
-            chosen = jnp.where(low_half, first_ref[0, z].astype(F32), second_ref[0, z].astype(F32))
-            crossed = jnp.where(low_half, second_ref[0, z].astype(F32), first_ref[0, z].astype(F32))
-            out_ref[z] = jnp.where(keep, chosen, pltpu.roll(crossed, EDGE, 1)).astype(BF16)
+    low_half = lane < EDGE
+    sides = ((below, 1, down_ref), (above, -1, up_ref))
+    views = [pick_view(fields, way, rank) for fields, way, _ in sides for rank in range(2)]
+
+    def copy(n, chunk):
+        return pltpu.make_async_copy(
+            volumes_ref.at[views[n], pl.ds(chunk * PCHUNK, PCHUNK)],
+            held.at[n, pl.ds(chunk * PCHUNK, PCHUNK)],
+            sems.at[n, chunk],
+        )
+
+    for chunk in range(EDGE // PCHUNK):
+        for n in range(4):
+            copy(n, chunk).start()
+
+    def weight(keep):
+        return jnp.where(keep, 1.0, 0.0).astype(BF16)
+
+    weights = []
+    for fields, way, _ in sides:
+        start_first, start_second = pick_start(fields, way, 0), pick_start(fields, way, 1)
+        weights.append(
+            (
+                weight(low_half & (lane >= start_first)),
+                weight(~low_half & (lane < start_second + EDGE)),
+                weight(~low_half & (lane < start_first + EDGE)),
+                weight(low_half & (lane >= start_second)),
+            )
+        )
+
+    def step(chunk, carry):
+        for n in range(4):
+            copy(n, chunk).wait()
+        for side, (_, _, out_ref) in enumerate(sides):
+            stay_first, stay_second, move_first, move_second = weights[side]
+            for k in range(PCHUNK):
+                z = chunk * PCHUNK + k
+                first, second = held[2 * side, z], held[2 * side + 1, z]
+                moved = pltpu.roll(first * move_first + second * move_second, EDGE, 1)
+                out_ref[z] = first * stay_first + second * stay_second + moved
+        return carry
+
+    lax.fori_loop(0, EDGE // PCHUNK, step, 0)
 
 
 def packed_blocks(volumes, below_fields, above_fields):
-    planes = 16
-    block = (1, planes, EDGE, LANES)
-
-    def taken(from_below, rank):
-        def index(i, below, above):
-            fields, direction = (below, 1) if from_below else (above, -1)
-            return pick_view(fields, direction, rank), i, 0, 0
-
-        return pl.BlockSpec(block, index)
-
-    out_block = pl.BlockSpec((planes, EDGE, LANES), lambda i, below, above: (i, 0, 0))
-    shape = jax.ShapeDtypeStruct((EDGE, EDGE, LANES), BF16)
+    whole = pl.BlockSpec(memory_space=pltpu.VMEM)
+    scalar = pl.BlockSpec(memory_space=pltpu.SMEM)
+    shape = pltpu.VMEM((EDGE, EDGE, LANES), BF16)
     return pl.pallas_call(
         pack_kernel,
         out_shape=(shape, shape),
-        grid_spec=pltpu.PrefetchScalarGridSpec(
-            num_scalar_prefetch=2,
-            grid=(EDGE // planes,),
-            in_specs=[taken(True, 0), taken(True, 1), taken(False, 0), taken(False, 1)],
-            out_specs=(out_block, out_block),
-        ),
+        in_specs=[scalar, scalar, pl.BlockSpec(memory_space=pl.ANY)],
+        out_specs=(whole, whole),
+        scratch_shapes=[
+            pltpu.VMEM((4, EDGE, EDGE, LANES), BF16),
+            pltpu.SemaphoreType.DMA((4, EDGE // PCHUNK)),
+        ],
+        compiler_params=pltpu.CompilerParams(vmem_limit_bytes=GRANT),
         name="pack",
-    )(below_fields, above_fields, volumes, volumes, volumes, volumes)
+    )(below_fields, above_fields, volumes)
 
 
 def first_spectra(volumes, pair_fields, x_tables, y_table):
     whole = pl.BlockSpec(memory_space=pltpu.VMEM)
     return pl.pallas_call(
         first_kernel,
-        out_shape=jax.ShapeDtypeStruct((EDGE, EDGE, 2 * LANES), F32),
+        out_shape=pltpu.VMEM((EDGE, EDGE, 2 * LANES), F32),
         in_specs=[
             pl.BlockSpec(memory_space=pltpu.SMEM),
             pl.BlockSpec(memory_space=pl.ANY),
@@ -614,36 +659,35 @@
             pltpu.VMEM((2, 2 * LANES, 2 * LANES), BF16),
             pltpu.SemaphoreType.DMA((SLOTS, EDGE // XCHUNK)),
         ],
+        compiler_params=pltpu.CompilerParams(vmem_limit_bytes=GRANT),
         name="first_spectra",
     )(pair_fields, volumes, x_tables, y_table)
 
 
-def correlated(volumes, above, below, grid_a, pair_fields, pair_counts, place, tables):
+def correlated(volumes, above, below, grid_a, pair_fields, tables):
     whole = pl.BlockSpec(memory_space=pltpu.VMEM)
     scalar = pl.BlockSpec(memory_space=pltpu.SMEM)
     left = pl.BlockSpec(memory_space=pl.ANY)
-    grid = pltpu.VMEM((EDGE, EDGE, 2 * LANES), F32)
     return pl.pallas_call(
         second_kernel,
         out_shape=(
-            jax.ShapeDtypeStruct((WIN * WIN, LANES), F32),
-            jax.ShapeDtypeStruct((ROWS, LANES), F32),
+            jax.ShapeDtypeStruct((SLOTS, WIN**3), F32),
+            jax.ShapeDtypeStruct((3, SLOTS), F32),
             jax.ShapeDtypeStruct((ROWS, LANES), F32),
         ),
-        in_specs=[scalar] * 3 + [left] * 4 + [whole] * 5,
+        in_specs=[scalar] + [left] * 3 + [whole] * 7,
         out_specs=(whole,) * 3,
         scratch_shapes=[
             pltpu.VMEM((SLOTS, EDGE, EDGE, LANES), BF16),
-            grid,
-            grid,
+            pltpu.VMEM((EDGE, EDGE, 2 * LANES), F32),
             pltpu.VMEM((HALF, 4, 4, ROWS, LANES), F32),
             pltpu.VMEM((2, EDGE, ROWS, LANES), F32),
             pltpu.VMEM((2, 2 * LANES, 2 * LANES), BF16),
             pltpu.SemaphoreType.DMA((SLOTS, EDGE // XCHUNK)),
-            pltpu.SemaphoreType.DMA,
         ],
+        compiler_params=pltpu.CompilerParams(vmem_limit_bytes=GRANT),
         name="correlated",
-    )(pair_fields, pair_counts, place, volumes, above, below, grid_a, *tables)
+    )(pair_fields, volumes, above, below, grid_a, *tables)
 
 
 def split_outside(values):
@@ -655,15 +699,20 @@
     slot = jnp.arange(EDGE, dtype=jnp.int32)
     freq = jnp.where(slot <= HALF, slot, slot - HALF)
     steps = jnp.arange(WIN, dtype=jnp.int32)
-    offsets = pair_fields[5:8] + jnp.array([[0], [0], [1]], jnp.int32) * (
-        pair_fields[1] - pair_fields[4]
-    )
-    where_at = offsets[:, :, None, None] + steps[None, None, :, None]
+    shift = pair_fields[:, 1:2] - pair_fields[:, 4:5]
+    offsets = pair_fields[:, 5:8] + jnp.where(jnp.arange(3) == 2, shift, 0)
+    where_at = jnp.transpose(offsets)[:, :, None, None] + steps[None, None, :, None]
     phase = jnp.mod(where_at * freq, EDGE) - jnp.where(slot <= HALF, 0, EDGE // 4)
     values = jnp.cos((2.0 * math.pi / EDGE) * phase.astype(F32))
     vz = jnp.repeat(jnp.transpose(values[0], (2, 1, 0)), HALF, axis=2)
     high, low = split_outside(values[1].reshape(SLOTS * WIN, EDGE))
-    vy = jnp.concatenate([high, high, low], axis=1)
+    vy = jnp.concatenate(
+        [
+            jnp.concatenate([high, high], axis=1),
+            jnp.concatenate([low, jnp.zeros_like(low)], axis=1),
+        ],
+        axis=0,
+    )
     live = (jnp.arange(SLOTS) < pair_counts[0]).astype(F32) * (2.0 / EDGE**1.5)
     vx = values[2] * live[:, None, None]
     vx = jnp.transpose(vx.reshape(SLOTS, WIN, 2, HALF), (2, 0, 3, 1))
@@ -674,53 +723,61 @@
     return vy, vz, jnp.concatenate([high, high, low], axis=0)
 
 
-def group_sum(part, axis, size, stride):
-    count = lax.axis_size(axis)
-    groups = [
+def groups_of(count, size, stride):
+    return [
         [base + first + stride * k for k in range(size)]
         for base in range(0, count, size * stride)
         for first in range(stride)
     ]
-    every = lax.all_gather(part, axis, axis=0, tiled=False, axis_index_groups=groups)
-    return jnp.sum(every, axis=0)
+
+
+def slab_total(part, axis):
+    count = lax.axis_size(axis)
+    reach = 1
+    for size in (2, 4):
+        if count % (reach * size):
+            break
+        groups = groups_of(count, size, reach)
+        if size == 2:
+            part = jnp.sum(
+                lax.all_gather(part, axis, axis=0, tiled=False, axis_index_groups=groups), axis=0
+            )
+        else:
+            part = lax.psum(part, axis, axis_index_groups=groups)
+        reach *= size
+    if reach < count:
+        part = lax.psum(part, axis, axis_index_groups=groups_of(count, count // reach, reach))
+    return part
 
 
 def on_device(volumes, pair_fields, pair_counts):
     view_count = volumes.shape[0]
     slab_count = lax.axis_size("slab")
-    own_index = lax.axis_index("slab")
+    volumes = pltpu.with_memory_space_constraint(volumes, pltpu.HBM)
+    pair_fields = jnp.transpose(pair_fields)
     below_fields = passed_along(pair_fields, "slab", 1)
     above_fields = passed_along(pair_fields, "slab", -1)
     down, up = packed_blocks(volumes, below_fields, above_fields)
-    from_above = passed_along(down, "slab", -1)
-    from_below = passed_along(up, "slab", 1)
+    late_fields, late_counts, down, up = lax.optimization_barrier(
+        (pair_fields, pair_counts, down, up)
+    )
+    from_above = pltpu.with_memory_space_constraint(passed_along(down, "slab", -1), pltpu.HBM)
+    from_below = pltpu.with_memory_space_constraint(passed_along(up, "slab", 1), pltpu.HBM)
     x_tables, y_table = jnp.asarray(x_tables_np()), jnp.asarray(y_table_np())
-    grid_a = first_spectra(volumes, pair_fields, x_tables, y_table)
-    vy, vz, vx = window_tables(pair_fields, pair_counts)
-    place = jnp.stack([own_index.astype(jnp.int32), jnp.int32(slab_count)])
+    grid_a = first_spectra(volumes, late_fields, x_tables, y_table)
+    windows = window_tables(late_fields, late_counts)
     corr, shift, part = correlated(
         volumes,
         from_above,
         from_below,
         grid_a,
-        pair_fields,
-        pair_counts,
-        place,
-        (x_tables, y_table, vy, vz, vx),
-    )
-    corr = jnp.transpose(corr[:, : SLOTS * WIN].reshape(WIN * WIN, SLOTS, WIN), (1, 0, 2))
-    corr = corr.reshape(SLOTS, WIN**3)
-    first = 1
-    while 2 * first * first <= slab_count:
-        first *= 2
-    while slab_count % first:
-        first -= 1
-    part = group_sum(part, "slab", first, 1)
-    part = group_sum(part, "slab", slab_count // first, first)
-    part = part * (1.0 / (SLOTS * slab_count))
-    normal = part[:view_count, :16].reshape(view_count, 4, 4)
-    rhs = part[:view_count, 16:28].reshape(view_count, 4, 3)
-    return corr, shift[:3, :SLOTS], normal, rhs
+        late_fields,
+        (x_tables, y_table, *windows, jnp.asarray(flat_table_np())),
+    )
+    part = jnp.transpose(slab_total(part, "slab") * (1.0 / (SLOTS * slab_count)))
+    normal = jnp.transpose(part[:16, :view_count].reshape(4, 4, view_count), (2, 0, 1))
+    rhs = jnp.transpose(part[16:28, :view_count].reshape(3, 4, view_count), (2, 1, 0))
+    return corr, shift, normal, rhs
 
 
 def solution(mesh):

time: 137 us -> 105 us (0.77)
  Pallas kernels: 38 us -> 26.3 us
  blocking collectives: 73.1 us -> 61.8 us
  local copies, waits for them, and re-layouts: 9.67 us -> 2.13 us
  other arithmetic: 4.3 us -> 0.91 us
  starting transfers between devices: 9.5 us -> 11 us
    all_gather x2 -> x1, blocking collectives: 73.1 us -> 5.37 us  [slab_total(): lax.all_gather(part, axis, axis=0, tiled=False, axis_index_groups=groups)]
    psum x0 -> x2, blocking collectives: none -> 56.4 us  [the longest x1 40 us: slab_total(): lax.psum(part, axis, axis_index_groups=groups_of(count, count // reach, r...]
    pallas_call x3, Pallas kernels: 38 us -> 26.3 us  [the longest x1 14.5 us: correlated(): pl.pallas_call(second_kernel, out_shape=(jax.ShapeDtypeStruct((SLOTS, WIN...]
    unnamed x12 -> x8, local copies, waits for them, and re-layouts: 4.59 us -> 0.02 us
    slice x4 -> x3, local copies, waits for them, and re-layouts: 2.84 us -> 0.83 us  [the longest x1 0.67 us: on_device(): part[:16, :view_count].reshape(4, 4, view_count)]
    ppermute x4, starting transfers between devices: 9.5 us -> 11 us  [passed_along(): lax.ppermute(value, axis, [(source, source + steps) for source in range(l...]
  transfers between devices with their start and end apart: 4 -> 4, of which waited for: 0 -> 1; matrix products, arithmetic and copies ran while one was open for 4% -> 1% of each run, Pallas kernels for 9% -> 8%
where the time goes in v2:
time: 105 us; the launch traced here: 104 us
  blocking collectives  61.8 us (59%)
  Pallas kernels  26.3 us (25%)
  starting transfers between devices  11 us (10%)
  local copies, waits for them, and re-layouts  2.13 us (2%)
  between operations  1.52 us (1%)
    psum x1, blocking collectives, slab_total(): lax.psum(part, axis, axis_index_groups=groups_of(count, count // reach, r...  40 us
    psum x1, blocking collectives, slab_total(): part = lax.psum(part, axis, axis_index_groups=groups)  16.4 us
    pallas_call x1, Pallas kernels, correlated(): pl.pallas_call(second_kernel, out_shape=(jax.ShapeDtypeStruct((SLOTS, WIN...  14.5 us
    ppermute x4, starting transfers between devices, passed_along(): lax.ppermute(value, axis, [(source, source + steps) for source in range(l...  11 us
    pallas_call x1, Pallas kernels, first_spectra(): pl.pallas_call(first_kernel, out_shape=pltpu.VMEM((EDGE, EDGE, 2 * LANES)...  7.96 us
    all_gather x1, blocking collectives, slab_total(): lax.all_gather(part, axis, axis=0, tiled=False, axis_index_groups=groups)  5.37 us
    pallas_call x1, Pallas kernels, packed_blocks(): pl.pallas_call(pack_kernel, out_shape=(shape, shape), in_specs=[scalar, s...  3.85 us
  transfers between devices with their start and end apart: 4, of which 1 were waited for; matrix products, arithmetic and copies ran while one was open for 1% of the time, Pallas kernels for 8%

profile of v2, /device:TPU:38, one launch (start us, length us, event | category | flops | bytes accessed | tf_op | source)
XLA Modules:
  0.0 104.0 jit_solution(16671540105526003542)
XLA Ops:
  0.6 0.0 copy-start.1
  0.6 0.0 copy-start
  0.7 0.0 copy-start.3
  0.7 1.4 %collective-permute-start.1 = (s32[4,8]{1,0:T(4,128)}, s32[4,8]{1,0:T(4,128)S(1)}, u32[]{:S(2)}, u32[]{:S(2)}) collective-permute-start(s32[4,8]{1,0:T(4,128)} %bitcast.31), channel_id=1, source_target_pairs={{1,0},{2,1},{3,2},{4,3},{5,4},{6,5},{7,6},{8,7},{9,8},{10,9},{11,1... | collective-permute-start | bytes 392 | tf_op jit(solution)/shard_map/ppermute | solution.py:30
  2.1 3.1 %collective-permute-start = (s32[4,8]{1,0:T(4,128)}, s32[4,8]{1,0:T(4,128)S(1)}, u32[]{:S(2)}, u32[]{:S(2)}) collective-permute-start(s32[4,8]{1,0:T(4,128)} %bitcast.32), channel_id=1, source_target_pairs={{0,1},{1,2},{2,3},{3,4},{4,5},{5,6},{6,7},{7,8},{8,9},{9,10},{10,1... | collective-permute-start | bytes 392 | tf_op jit(solution)/shard_map/ppermute | solution.py:30
  5.9 0.0 collective-permute-done.1.above
  5.9 0.3 collective-permute-done.below
  6.2 3.8 %pack.1 = (bf16[64,64,128]{2,1,0:T(8,128)(2,1)S(1)}, bf16[64,64,128]{2,1,0:T(8,128)(2,1)S(1)}) custom-call(s32[4,8]{1,0:T(4,128)S(1)} %collective-permute-done.below, s32[4,8]{1,0:T(4,128)S(1)} %collective-permute-done.1.above, bf16[8,64,64,128]{3,2,1,0:T(8,128)(2,1)} %volumes_ref.5), custom_call_target="tpu_custom_call" | custom-call | tf_op jit(solution)/shard_map/pack/pallas_call | solution.py:630
  10.1 0.0 copy-start.2
  10.1 0.0 copy-done.3
  10.1 0.2 subtract_reduce_fusion
  10.3 0.1 add_bitcast_fusion
  10.3 0.1 copy.32
  10.4 0.1 iota_add_fusion
  10.5 1.3 %collective-permute-start.2 = (bf16[64,64,128]{2,1,0:T(8,128)(2,1)S(1)}, bf16[64,64,128]{2,1,0:T(8,128)(2,1)}, u32[]{:S(2)}, u32[]{:S(2)}) collective-permute-start(bf16[64,64,128]{2,1,0:T(8,128)(2,1)S(1)} %get-tuple-element.16), channel_id=1, source_target_pairs={{1,0},{2,1},{3,2},{4,3},{5,4},{6,5},{7,6},{8,7},{9,8},{10,9},{11,1... | collective-permute-start | bytes 3145736 | tf_op jit(solution)/shard_map/ppermute | solution.py:30
  11.8 5.2 %collective-permute-start.3 = (bf16[64,64,128]{2,1,0:T(8,128)(2,1)S(1)}, bf16[64,64,128]{2,1,0:T(8,128)(2,1)}, u32[]{:S(2)}, u32[]{:S(2)}) collective-permute-start(bf16[64,64,128]{2,1,0:T(8,128)(2,1)S(1)} %get-tuple-element.17), channel_id=1, source_target_pairs={{0,1},{1,2},{2,3},{3,4},{4,5},{5,6},{6,7},{7,8},{8,9},{9,10},{10,1... | collective-permute-start | bytes 3145736 | tf_op jit(solution)/shard_map/ppermute | solution.py:30
  17.0 0.3 fusion.4
  17.3 0.1 squeeze.10
  17.4 0.1 fusion.6
  17.5 0.1 broadcast_multiply_fusion
  17.6 0.1 mul.65
  17.7 0.1 copy.36
  17.8 0.2 copy.37.vz_ref
  18.1 0.0 copy-done.1
  18.1 0.0 copy-done
  18.1 8.0 %first_spectra.1.grid_a = f32[64,64,256]{2,1,0:T(8,128)S(1)} custom-call(s32[4,8]{1,0:T(4,128)S(1)} %bitcast.35, bf16[8,64,64,128]{3,2,1,0:T(8,128)(2,1)} %volumes_ref.5, bf16[2,256,256]{2,1,0:T(8,128)(2,1)S(1)} %copy-done, bf16[128,128]{1,0:T(8,128)(2,1)S(1)} %copy-done.1), custom_call_target="tpu_custom_call" | custom-call | tf_op jit(solution)/shard_map/first_spectra/pallas_call | solution.py:646
  26.1 0.1 fusion.9.vy_ref
  26.2 0.0 collective-permute-done.2.above_ref
  26.2 0.0 collective-permute-done.3.below_ref
  26.2 0.0 copy-done.2
  26.2 14.5 %correlated.1 = (f32[4,512]{1,0:T(4,128)}, f32[3,4]{1,0:T(4,128)}, f32[8,128]{1,0:T(8,128)S(1)}) custom-call(s32[4,8]{1,0:T(4,128)S(1)} %bitcast.36, bf16[8,64,64,128]{3,2,1,0:T(8,128)(2,1)} %volumes_ref.5, bf16[64,64,128]{2,1,0:T(8,128)(2,1)} %collective-permute-done.2.above_ref, bf16[64,64,128]{2,1,0:T(8,128)(2,1)} %collective-permute-done.3.below_ref, ...), custom_call_target="tpu_custom_call" | custom-call | tf_op jit(solution)/shard_map/correlated/pallas_call | solution.py:671
  40.7 5.4 %all-gather = f32[16,128]{1,0:T(8,128)S(1)} all-gather(f32[8,128]{1,0:T(8,128)S(1)} %get-tuple-element.21), channel_id=2, replica_groups={{0,1},{2,3},{4,5},{6,7},{8,9},{10,11},{12,13},{14,15},{16,17},{18,19},{..., dimensions={0}, use_global_device_ids=true | all-gather | bytes 12288 | tf_op jit(solution)/shard_map/all_gather | solution.py:743
  46.1 16.4 %psum.14 = f32[8,128]{1,0:T(8,128)S(1)} all-reduce(f32[8,128]{1,0:T(8,128)S(1)} %bitcast_reduce_fusion), channel_id=1, replica_groups={{0,2,4,6},{1,3,5,7},{8,10,12,14},{9,11,13,15},{16,18,20,22},{17,19,21,2..., use_global_device_ids=true, to_apply=%region_1.2 | all-reduce | flops 1024 | bytes 8192 | tf_op jit(solution)/shard_map/psum | solution.py:746
  62.5 40.0 %psum.15 = f32[8,128]{1,0:T(8,128)S(1)} all-reduce(f32[8,128]{1,0:T(8,128)S(1)} %psum.14), channel_id=1, replica_groups={{0,8,16,24,32,40,48,56},{1,9,17,25,33,41,49,57},{2,10,18,26,34,42,50,58..., use_global_device_ids=true, to_apply=%region_2.3 | all-reduce | flops 1024 | bytes 8192 | tf_op jit(solution)/shard_map/psum | solution.py:749
  102.5 0.1 slice.31
  102.6 0.1 copy.39
  102.7 0.6 reshape.59
  103.3 0.7 copy.38
  (13 shorter events, 0.1 us)
Async XLA Ops:
  0.6 17.4 %copy-start.1 = (bf16[128,128]{1,0:T(8,128)(2,1)S(1)}, bf16[128,128]{1,0:T(8,128)(2,1)}, u32[]{:S(2)}) copy-start(bf16[128,128]{1,0:T(8,128)(2,1)} %constant.42.clone.y_table_ref) | copy-start | bytes 98308
  0.6 17.4 %copy-start = (bf16[2,256,256]{2,1,0:T(8,128)(2,1)S(1)}, bf16[2,256,256]{2,1,0:T(8,128)(2,1)}, u32[]{:S(2)}) copy-start(bf16[2,256,256]{2,1,0:T(8,128)(2,1)} %constant.41.clone.x_table_ref) | copy-start | bytes 786436
  0.7 9.4 %copy-start.3 = (s32[8,4]{0,1:T(4,128)S(1)}, s32[8,4]{0,1:T(4,128)}, u32[]{:S(2)}) copy-start(s32[8,4]{0,1:T(4,128)} %param.7) | copy-start | bytes 388
  0.7 5.2 %collective-permute-start.1 = (s32[4,8]{1,0:T(4,128)}, s32[4,8]{1,0:T(4,128)S(1)}, u32[]{:S(2)}, u32[]{:S(2)}) collective-permute-start(s32[4,8]{1,0:T(4,128)} %bitcast.31), channel_id=1, source_target_pairs={{1,0},{2,1},{3,2},{4,3},{5,4},{6,5},{7,6},{8,7},{9,8},{10,9},{11,1... | collective-permute-start | bytes 392 | tf_op jit(solution)/shard_map/ppermute | solution.py:30
  2.1 4.1 %collective-permute-start = (s32[4,8]{1,0:T(4,128)}, s32[4,8]{1,0:T(4,128)S(1)}, u32[]{:S(2)}, u32[]{:S(2)}) collective-permute-start(s32[4,8]{1,0:T(4,128)} %bitcast.32), channel_id=1, source_target_pairs={{0,1},{1,2},{2,3},{3,4},{4,5},{5,6},{6,7},{7,8},{8,9},{9,10},{10,1... | collective-permute-start | bytes 392 | tf_op jit(solution)/shard_map/ppermute | solution.py:30
  10.1 16.2 %copy-start.2 = (bf16[96,512]{1,0:T(8,128)(2,1)S(1)}, bf16[96,512]{1,0:T(8,128)(2,1)}, u32[]{:S(2)}) copy-start(bf16[96,512]{1,0:T(8,128)(2,1)} %constant.43.clone.flat_ref) | copy-start | bytes 294916
  10.5 15.7 %collective-permute-start.2 = (bf16[64,64,128]{2,1,0:T(8,128)(2,1)S(1)}, bf16[64,64,128]{2,1,0:T(8,128)(2,1)}, u32[]{:S(2)}, u32[]{:S(2)}) collective-permute-start(bf16[64,64,128]{2,1,0:T(8,128)(2,1)S(1)} %get-tuple-element.16), channel_id=1, source_target_pairs={{1,0},{2,1},{3,2},{4,3},{5,4},{6,5},{7,6},{8,7},{9,8},{10,9},{11,1... | collective-permute-start | bytes 3145736 | tf_op jit(solution)/shard_map/ppermute | solution.py:30
  11.8 14.4 %collective-permute-start.3 = (bf16[64,64,128]{2,1,0:T(8,128)(2,1)S(1)}, bf16[64,64,128]{2,1,0:T(8,128)(2,1)}, u32[]{:S(2)}, u32[]{:S(2)}) collective-permute-start(bf16[64,64,128]{2,1,0:T(8,128)(2,1)S(1)} %get-tuple-element.17), channel_id=1, source_target_pairs={{0,1},{1,2},{2,3},{3,4},{4,5},{5,6},{6,7},{7,8},{8,9},{9,10},{10,1... | collective-permute-start | bytes 3145736 | tf_op jit(solution)/shard_map/ppermute | solution.py:30

commit v3 on v2

--- a/solution.py
+++ b/solution.py
@@ -1,3 +1,4 @@
+import functools
 import math
 
 import jax
@@ -8,8 +9,10 @@
 from jax.experimental.pallas import tpu as pltpu
 from jax.sharding import PartitionSpec as P
 
+
 WIN = 8
 EPSILON = 1e-06
+TINY = 1e-37
 SLOTS = 4
 EDGE = 64
 HALF = 32
@@ -24,10 +27,13 @@
 BF16 = jnp.bfloat16
 
 
-def passed_along(value, axis, steps):
-    count = lax.axis_size(axis)
-    leading, last = (max(0, -steps), min(count, count - steps))
-    return lax.ppermute(value, axis, [(source, source + steps) for source in range(leading, last)])
+def swapped(value, axis, first):
+    pairs = [(low, low + 1) for low in range(first, lax.axis_size(axis) - 1, 2)]
+    return lax.ppermute(value, axis, pairs + [(high, low) for low, high in pairs])
+
+
+def partner_way():
+    return 1 - 2 * (lax.axis_index("slab") % 2)
 
 
 def basis_np():
@@ -61,8 +67,7 @@
 
 def y_table_np():
     high, low = split_np(basis_np().T)
-    above = np.concatenate([high, high], axis=1)
-    return np.concatenate([above, np.concatenate([low, np.zeros_like(low)], axis=1)], axis=0)
+    return np.concatenate([high, high, low], axis=1)
 
 
 def split(values):
@@ -210,10 +215,11 @@
         for k in range(Y_UNROLL):
             z = step * Y_UNROLL + k
             high, low = split(grid_ref[z])
-            both = jnp.dot(
-                y_table_ref[...], jnp.concatenate([high, low], axis=0), preferred_element_type=F32
+            grid_ref[z] = jnp.dot(
+                y_table_ref[...],
+                jnp.concatenate([high, low, high], axis=0),
+                preferred_element_type=F32,
             )
-            grid_ref[z] = both[:EDGE] + both[EDGE:]
         return carry
 
     lax.fori_loop(0, EDGE // Y_UNROLL, y_step, 0)
@@ -298,7 +304,8 @@
                 cr, ci = rr + ii, ai * br - ar * bi
                 if z_zero and tile == 0:
                     cr, ci = jnp.where(corner, rr, cr), jnp.where(corner, ii, ci)
-                size = jnp.sqrt(cr * cr + ci * ci)
+                square = cr * cr + ci * ci
+                size = square * lax.rsqrt(jnp.maximum(square, TINY))
                 counted = size
                 if z_zero and tile == 0:
                     counted = jnp.where(corner, 0.5 * (jnp.abs(cr) + jnp.abs(ci)), size)
@@ -443,8 +450,8 @@
 def second_kernel(
     fields,
     volumes_ref,
-    above_ref,
-    below_ref,
+    partner_ref,
+    cross_ref,
     grid_a,
     x_table_ref,
     y_table_ref,
@@ -471,10 +478,12 @@
             sems.at[p, chunk],
         )
 
+    way = partner_way()
     for chunk in range(chunks):
         for p in range(SLOTS):
             side = fields[p, 3]
-            for value, source in ((0, volumes_ref.at[fields[p, 2]]), (1, above_ref), (-1, below_ref)):
+            local = volumes_ref.at[fields[p, 2]]
+            for value, source in ((0, local), (way, partner_ref), (-way, cross_ref)):
 
                 @pl.when(side == value)
                 def _(source=source):
@@ -482,7 +491,7 @@
 
     def wait_chunk(chunk):
         for p in range(SLOTS):
-            copy_from(above_ref, p, chunk).wait()
+            copy_from(partner_ref, p, chunk).wait()
 
     starts = []
     for p in range(SLOTS):
@@ -576,11 +585,11 @@
     return start
 
 
-def pack_kernel(below, above, volumes_ref, down_ref, up_ref, held, sems):
+def pack_kernel(toward, fields, volumes_ref, out_ref, held, sems):
     lane = lax.broadcasted_iota(jnp.int32, (EDGE, LANES), 1)
     low_half = lane < EDGE
-    sides = ((below, 1, down_ref), (above, -1, up_ref))
-    views = [pick_view(fields, way, rank) for fields, way, _ in sides for rank in range(2)]
+    way = toward * partner_way()
+    views = [pick_view(fields, way, rank) for rank in range(2)]
 
     def copy(n, chunk):
         return pltpu.make_async_copy(
@@ -590,55 +599,44 @@
         )
 
     for chunk in range(EDGE // PCHUNK):
-        for n in range(4):
+        for n in range(2):
             copy(n, chunk).start()
 
     def weight(keep):
         return jnp.where(keep, 1.0, 0.0).astype(BF16)
 
-    weights = []
-    for fields, way, _ in sides:
-        start_first, start_second = pick_start(fields, way, 0), pick_start(fields, way, 1)
-        weights.append(
-            (
-                weight(low_half & (lane >= start_first)),
-                weight(~low_half & (lane < start_second + EDGE)),
-                weight(~low_half & (lane < start_first + EDGE)),
-                weight(low_half & (lane >= start_second)),
-            )
-        )
+    start_first, start_second = pick_start(fields, way, 0), pick_start(fields, way, 1)
+    stay_first = weight(low_half & (lane >= start_first))
+    stay_second = weight(~low_half & (lane < start_second + EDGE))
+    move_first = weight(~low_half & (lane < start_first + EDGE))
+    move_second = weight(low_half & (lane >= start_second))
 
     def step(chunk, carry):
-        for n in range(4):
+        for n in range(2):
             copy(n, chunk).wait()
-        for side, (_, _, out_ref) in enumerate(sides):
-            stay_first, stay_second, move_first, move_second = weights[side]
-            for k in range(PCHUNK):
-                z = chunk * PCHUNK + k
-                first, second = held[2 * side, z], held[2 * side + 1, z]
-                moved = pltpu.roll(first * move_first + second * move_second, EDGE, 1)
-                out_ref[z] = first * stay_first + second * stay_second + moved
+        for k in range(PCHUNK):
+            z = chunk * PCHUNK + k
+            first, second = held[0, z], held[1, z]
+            moved = pltpu.roll(first * move_first + second * move_second, EDGE, 1)
+            out_ref[z] = first * stay_first + second * stay_second + moved
         return carry
 
     lax.fori_loop(0, EDGE // PCHUNK, step, 0)
 
 
-def packed_blocks(volumes, below_fields, above_fields):
+def packed_blocks(volumes, fields, toward):
     whole = pl.BlockSpec(memory_space=pltpu.VMEM)
-    scalar = pl.BlockSpec(memory_space=pltpu.SMEM)
-    shape = pltpu.VMEM((EDGE, EDGE, LANES), BF16)
     return pl.pallas_call(
-        pack_kernel,
-        out_shape=(shape, shape),
-        in_specs=[scalar, scalar, pl.BlockSpec(memory_space=pl.ANY)],
-        out_specs=(whole, whole),
+        functools.partial(pack_kernel, toward),
+        out_shape=pltpu.VMEM((EDGE, EDGE, LANES), BF16),
+        in_specs=[pl.BlockSpec(memory_space=pltpu.SMEM), pl.BlockSpec(memory_space=pl.ANY)],
+        out_specs=whole,
         scratch_shapes=[
-            pltpu.VMEM((4, EDGE, EDGE, LANES), BF16),
-            pltpu.SemaphoreType.DMA((4, EDGE // PCHUNK)),
+            pltpu.VMEM((2, EDGE, EDGE, LANES), BF16),
+            pltpu.SemaphoreType.DMA((2, EDGE // PCHUNK)),
         ],
         compiler_params=pltpu.CompilerParams(vmem_limit_bytes=GRANT),
-        name="pack",
-    )(below_fields, above_fields, volumes)
+    )(fields, volumes)
 
 
 def first_spectra(volumes, pair_fields, x_tables, y_table):
@@ -664,7 +662,7 @@
     )(pair_fields, volumes, x_tables, y_table)
 
 
-def correlated(volumes, above, below, grid_a, pair_fields, tables):
+def correlated(volumes, from_partner, from_cross, grid_a, pair_fields, tables):
     whole = pl.BlockSpec(memory_space=pltpu.VMEM)
     scalar = pl.BlockSpec(memory_space=pltpu.SMEM)
     left = pl.BlockSpec(memory_space=pl.ANY)
@@ -687,7 +685,7 @@
         ],
         compiler_params=pltpu.CompilerParams(vmem_limit_bytes=GRANT),
         name="correlated",
-    )(pair_fields, volumes, above, below, grid_a, *tables)
+    )(pair_fields, volumes, from_partner, from_cross, grid_a, *tables)
 
 
 def split_outside(values):
@@ -755,21 +753,24 @@
     slab_count = lax.axis_size("slab")
     volumes = pltpu.with_memory_space_constraint(volumes, pltpu.HBM)
     pair_fields = jnp.transpose(pair_fields)
-    below_fields = passed_along(pair_fields, "slab", 1)
-    above_fields = passed_along(pair_fields, "slab", -1)
-    down, up = packed_blocks(volumes, below_fields, above_fields)
-    late_fields, late_counts, down, up = lax.optimization_barrier(
-        (pair_fields, pair_counts, down, up)
-    )
-    from_above = pltpu.with_memory_space_constraint(passed_along(down, "slab", -1), pltpu.HBM)
-    from_below = pltpu.with_memory_space_constraint(passed_along(up, "slab", 1), pltpu.HBM)
+    cross_fields = swapped(pair_fields, "slab", 1)
+    partner_fields = swapped(pair_fields, "slab", 0)
+    for_cross = packed_blocks(volumes, cross_fields, 1)
+    from_cross = swapped(for_cross, "slab", 1)
+    from_cross = pltpu.with_memory_space_constraint(from_cross, pltpu.HBM)
+    partner_fields, for_cross = lax.optimization_barrier((partner_fields, for_cross))
+    for_partner = packed_blocks(volumes, partner_fields, -1)
+    from_partner = pltpu.with_memory_space_constraint(swapped(for_partner, "slab", 0), pltpu.HBM)
+    late_fields, late_counts, for_partner = lax.optimization_barrier(
+        (pair_fields, pair_counts, for_partner)
+    )
     x_tables, y_table = jnp.asarray(x_tables_np()), jnp.asarray(y_table_np())
     grid_a = first_spectra(volumes, late_fields, x_tables, y_table)
     windows = window_tables(late_fields, late_counts)
     corr, shift, part = correlated(
         volumes,
-        from_above,
-        from_below,
+        from_partner,
+        from_cross,
         grid_a,
         late_fields,
         (x_tables, y_table, *windows, jnp.asarray(flat_table_np())),
@@ -788,6 +789,7 @@
         P("tm", None, None),
         P("tm", None, None),
     )
+
     return jax.shard_map(
         on_device, mesh=mesh, in_specs=in_specs, out_specs=out_specs, check_vma=False
     )

time: 105 us -> 101 us (0.962)
  starting transfers between devices: 11 us -> 6.59 us
    ppermute x4, starting transfers between devices: 11 us -> 6.59 us  [swapped(): lax.ppermute(value, axis, pairs + [(high, low) for low, high in pairs])]
    all_gather x1, blocking collectives: 5.37 us -> 7.16 us  [slab_total(): lax.all_gather(part, axis, axis=0, tiled=False, axis_index_groups=groups)]
    pallas_call x1 -> x2, Pallas kernels: 3.85 us -> 5.33 us  [packed_blocks(): pl.pallas_call(functools.partial(pack_kernel, toward), out_shape=pltpu.VM...]
  transfers between devices with their start and end apart: 4 -> 4, of which waited for: 1 -> 0; matrix products, arithmetic and copies ran while one was open for 1% -> 2% of each run, Pallas kernels for 8% -> 10%
where the time goes in v3:
time: 101 us
  blocking collectives  62.2 us (62%)
  Pallas kernels  27.3 us (27%)
  starting transfers between devices  6.59 us (7%)
  local copies, waits for them, and re-layouts  2.13 us (2%)
  between operations  1.5 us (1%)
    psum x1, blocking collectives, slab_total(): lax.psum(part, axis, axis_index_groups=groups_of(count, count // reach, r...  39 us
    psum x1, blocking collectives, slab_total(): part = lax.psum(part, axis, axis_index_groups=groups)  16 us
    pallas_call x1, Pallas kernels, correlated(): pl.pallas_call(second_kernel, out_shape=(jax.ShapeDtypeStruct((SLOTS, WIN...  14.2 us
    pallas_call x1, Pallas kernels, first_spectra(): pl.pallas_call(first_kernel, out_shape=pltpu.VMEM((EDGE, EDGE, 2 * LANES)...  7.74 us
    all_gather x1, blocking collectives, slab_total(): lax.all_gather(part, axis, axis=0, tiled=False, axis_index_groups=groups)  7.16 us
    ppermute x4, starting transfers between devices, swapped(): lax.ppermute(value, axis, pairs + [(high, low) for low, high in pairs])  6.59 us
    pallas_call x2, Pallas kernels, packed_blocks(): pl.pallas_call(functools.partial(pack_kernel, toward), out_shape=pltpu.VM...  5.33 us
  transfers between devices with their start and end apart: 4, of which 0 were waited for; matrix products, arithmetic and copies ran while one was open for 2% of the time, Pallas kernels for 10%

profile of v3, /device:TPU:38, one launch (start us, length us, event | category | flops | bytes accessed | tf_op | source)
XLA Modules:
  0.0 100.6 jit_solution(17653917199540462749)
XLA Ops:
  0.6 0.7 collective-permute-start.1
  1.3 3.6 %collective-permute-start = (s32[4,8]{1,0:T(4,128)}, s32[4,8]{1,0:T(4,128)S(1)}, u32[]{:S(2)}, u32[]{:S(2)}) collective-permute-start(s32[4,8]{1,0:T(4,128)} %bitcast.32), channel_id=1, source_target_pairs={{0,1},{2,3},{4,5},{6,7},{8,9},{10,11},{12,13},{14,15},{16,17},{18,... | collective-permute-start | bytes 392 | tf_op jit(solution)/shard_map/ppermute | solution.py:32
  5.6 0.0 copy-start.3
  5.6 0.0 copy-start
  5.6 0.0 copy-start.1
  5.7 0.0 collective-permute-done.1.fields
  5.7 2.7 %shard_map.93 = bf16[64,64,128]{2,1,0:T(8,128)(2,1)S(1)} custom-call(s32[4,8]{1,0:T(4,128)S(1)} %collective-permute-done.1.fields, bf16[8,64,64,128]{3,2,1,0:T(8,128)(2,1)} %volumes_ref.7), custom_call_target="tpu_custom_call" | custom-call | tf_op jit(solution)/shard_map/pallas_call | solution.py:629
  8.4 0.0 collective-permute-done.fields
  8.4 2.6 %shard_map.94 = bf16[64,64,128]{2,1,0:T(8,128)(2,1)S(1)} custom-call(s32[4,8]{1,0:T(4,128)S(1)} %collective-permute-done.fields, bf16[8,64,64,128]{3,2,1,0:T(8,128)(2,1)} %volumes_ref.7), custom_call_target="tpu_custom_call" | custom-call | tf_op jit(solution)/shard_map/pallas_call | solution.py:629
  11.0 0.0 copy-start.2
  11.0 0.6 collective-permute-start.2
  11.6 1.7 %collective-permute-start.3 = (bf16[64,64,128]{2,1,0:T(8,128)(2,1)S(1)}, bf16[64,64,128]{2,1,0:T(8,128)(2,1)}, u32[]{:S(2)}, u32[]{:S(2)}) collective-permute-start(bf16[64,64,128]{2,1,0:T(8,128)(2,1)S(1)} %shard_map.93), channel_id=1, source_target_pairs={{1,2},{3,4},{5,6},{7,8},{9,10},{11,12},{13,14},{15,16},{17,18},{19... | collective-permute-start | bytes 3145736 | tf_op jit(solution)/shard_map/ppermute | solution.py:32
  13.3 0.0 copy-done.3
  13.3 0.2 subtract_reduce_fusion
  13.5 0.1 add_bitcast_fusion
  13.6 0.1 copy.32
  13.7 0.1 iota_add_fusion
  13.8 0.3 fusion.4
  14.1 0.1 squeeze.10
  14.1 0.1 fusion.6
  14.2 0.1 broadcast_multiply_fusion
  14.3 0.1 mul.65
  14.5 0.1 copy.36
  14.6 0.2 copy.37.vz_ref
  14.8 0.0 copy-done
  14.8 0.0 copy-done.1
  14.8 7.7 %first_spectra.1.grid_a = f32[64,64,256]{2,1,0:T(8,128)S(1)} custom-call(s32[4,8]{1,0:T(4,128)S(1)} %bitcast.35, bf16[8,64,64,128]{3,2,1,0:T(8,128)(2,1)} %volumes_ref.7, bf16[2,256,256]{2,1,0:T(8,128)(2,1)S(1)} %copy-done, bf16[64,192]{1,0:T(8,128)(2,1)S(1)} %copy-done.1), custom_call_target="tpu_custom_call" | custom-call | tf_op jit(solution)/shard_map/first_spectra/pallas_call | solution.py:644
  22.6 0.1 fusion.9.vy_ref
  22.7 0.0 collective-permute-done.2.partner_ref
  22.7 0.0 collective-permute-done.3.cross_ref
  22.8 0.0 copy-done.2
  22.8 14.2 %correlated.1 = (f32[4,512]{1,0:T(4,128)}, f32[3,4]{1,0:T(4,128)}, f32[8,128]{1,0:T(8,128)S(1)}) custom-call(s32[4,8]{1,0:T(4,128)S(1)} %bitcast.36, bf16[8,64,64,128]{3,2,1,0:T(8,128)(2,1)} %volumes_ref.7, bf16[64,64,128]{2,1,0:T(8,128)(2,1)} %collective-permute-done.2.partner_ref, bf16[64,64,128]{2,1,0:T(8,128)(2,1)} %collective-permute-done.3.cross_ref, ...), custom_call_target="tpu_custom_call" | custom-call | tf_op jit(solution)/shard_map/correlated/pallas_call | solution.py:669
  37.0 7.2 %all-gather = f32[16,128]{1,0:T(8,128)S(1)} all-gather(f32[8,128]{1,0:T(8,128)S(1)} %get-tuple-element.15), channel_id=2, replica_groups={{0,1},{2,3},{4,5},{6,7},{8,9},{10,11},{12,13},{14,15},{16,17},{18,19},{..., dimensions={0}, use_global_device_ids=true | all-gather | bytes 12288 | tf_op jit(solution)/shard_map/all_gather | solution.py:741
  44.2 16.0 %psum.14 = f32[8,128]{1,0:T(8,128)S(1)} all-reduce(f32[8,128]{1,0:T(8,128)S(1)} %bitcast_reduce_fusion), channel_id=1, replica_groups={{0,2,4,6},{1,3,5,7},{8,10,12,14},{9,11,13,15},{16,18,20,22},{17,19,21,2..., use_global_device_ids=true, to_apply=%region_1.2 | all-reduce | flops 1024 | bytes 8192 | tf_op jit(solution)/shard_map/psum | solution.py:744
  60.1 39.0 %psum.15 = f32[8,128]{1,0:T(8,128)S(1)} all-reduce(f32[8,128]{1,0:T(8,128)S(1)} %psum.14), channel_id=1, replica_groups={{0,8,16,24,32,40,48,56},{1,9,17,25,33,41,49,57},{2,10,18,26,34,42,50,58..., use_global_device_ids=true, to_apply=%region_2.3 | all-reduce | flops 1024 | bytes 8192 | tf_op jit(solution)/shard_map/psum | solution.py:747
  99.2 0.1 slice.31
  99.3 0.1 copy.39
  99.4 0.6 reshape.59
  100.0 0.7 copy.38
  (13 shorter events, 0.1 us)
Async XLA Ops:
  0.6 5.0 %collective-permute-start.1 = (s32[4,8]{1,0:T(4,128)}, s32[4,8]{1,0:T(4,128)S(1)}, u32[]{:S(2)}, u32[]{:S(2)}) collective-permute-start(s32[4,8]{1,0:T(4,128)} %bitcast.31), channel_id=1, source_target_pairs={{1,2},{3,4},{5,6},{7,8},{9,10},{11,12},{13,14},{15,16},{17,18},{19... | collective-permute-start | bytes 392 | tf_op jit(solution)/shard_map/ppermute | solution.py:32
  1.3 7.1 %collective-permute-start = (s32[4,8]{1,0:T(4,128)}, s32[4,8]{1,0:T(4,128)S(1)}, u32[]{:S(2)}, u32[]{:S(2)}) collective-permute-start(s32[4,8]{1,0:T(4,128)} %bitcast.32), channel_id=1, source_target_pairs={{0,1},{2,3},{4,5},{6,7},{8,9},{10,11},{12,13},{14,15},{16,17},{18,... | collective-permute-start | bytes 392 | tf_op jit(solution)/shard_map/ppermute | solution.py:32
  5.6 7.7 %copy-start.3 = (s32[8,4]{0,1:T(4,128)S(1)}, s32[8,4]{0,1:T(4,128)}, u32[]{:S(2)}) copy-start(s32[8,4]{0,1:T(4,128)} %param.7) | copy-start | bytes 388
  5.6 9.2 %copy-start = (bf16[2,256,256]{2,1,0:T(8,128)(2,1)S(1)}, bf16[2,256,256]{2,1,0:T(8,128)(2,1)}, u32[]{:S(2)}) copy-start(bf16[2,256,256]{2,1,0:T(8,128)(2,1)} %constant.41.clone.x_table_ref) | copy-start | bytes 786436
  5.6 9.2 %copy-start.1 = (bf16[64,192]{1,0:T(8,128)(2,1)S(1)}, bf16[64,192]{1,0:T(8,128)(2,1)}, u32[]{:S(2)}) copy-start(bf16[64,192]{1,0:T(8,128)(2,1)} %constant.42.clone.y_table_ref) | copy-start | bytes 73732
  11.0 11.7 %copy-start.2 = (bf16[96,512]{1,0:T(8,128)(2,1)S(1)}, bf16[96,512]{1,0:T(8,128)(2,1)}, u32[]{:S(2)}) copy-start(bf16[96,512]{1,0:T(8,128)(2,1)} %constant.43.clone.flat_ref) | copy-start | bytes 294916
  11.0 11.7 %collective-permute-start.2 = (bf16[64,64,128]{2,1,0:T(8,128)(2,1)S(1)}, bf16[64,64,128]{2,1,0:T(8,128)(2,1)}, u32[]{:S(2)}, u32[]{:S(2)}) collective-permute-start(bf16[64,64,128]{2,1,0:T(8,128)(2,1)S(1)} %shard_map.94), channel_id=1, source_target_pairs={{0,1},{2,3},{4,5},{6,7},{8,9},{10,11},{12,13},{14,15},{16,17},{18,... | collective-permute-start | bytes 3145736 | tf_op jit(solution)/shard_map/ppermute | solution.py:32
  11.6 11.1 %collective-permute-start.3 = (bf16[64,64,128]{2,1,0:T(8,128)(2,1)S(1)}, bf16[64,64,128]{2,1,0:T(8,128)(2,1)}, u32[]{:S(2)}, u32[]{:S(2)}) collective-permute-start(bf16[64,64,128]{2,1,0:T(8,128)(2,1)S(1)} %shard_map.93), channel_id=1, source_target_pairs={{1,2},{3,4},{5,6},{7,8},{9,10},{11,12},{13,14},{15,16},{17,18},{19... | collective-permute-start | bytes 3145736 | tf_op jit(solution)/shard_map/ppermute | solution.py:32
